TPU v7x, 256 devices: a 4x2x16 block of a 4x16x16 slice. The times are simulated.
256 devices in a mesh: rep: 2 (over y), ep: 128 (over x, z, core).
Axes of the slice: x: 4, y: 2, z: 16, core: 2. Of those that a mesh axis runs over, the one named last changes fastest.
The devices are a block of a 4x16x16 slice.
Arguments:
- cache_kv: bfloat16 [512, 2048, 576], P(('rep', 'ep')), parts along dimension 0, may hold values from -6 to 6
- new_kv: bfloat16 [512, 2, 576], P(('rep', 'ep')), parts along dimension 0, may hold values from -6 to 6
- queries: bfloat16 [512, 2, 64, 576], P(('rep', 'ep')), parts along dimension 0, may hold values from -256 to 256
- lengths: int32 [512], P(('rep', 'ep')), parts along dimension 0, may hold values from 256 to 2048
- resid: bfloat16 [512, 2, 7168], P(('rep', 'ep')), parts along dimension 0, may hold values from -18 to 18
- value_up: bfloat16 [512, 8192], P(None, 'ep'), may hold values from -1.5 to 1.5
- out_proj: bfloat16 [8192, 7168], P('ep'), may hold values from -0.09375 to 0.09375
- norm_gain: bfloat16 [7168], replicated, may hold values from 0.25 to 1.75
- router: bfloat16 [7168, 16], replicated, may hold values from -0.0625 to 0.0625
- expert_ids: int32 [512, 2, 8], P(('rep', 'ep')), parts along dimension 0, may hold values from 0 to 15, as said below
- slots: int32 [512, 2, 8], P(('rep', 'ep')), parts along dimension 0, may hold values from 0 to 3, as said below
- w_gate: bfloat16 [7168, 16384], P(None, 'ep'), may hold values from -0.0625 to 0.0625
- w_up: bfloat16 [7168, 16384], P(None, 'ep'), may hold values from -0.0625 to 0.0625
- w_down: bfloat16 [16384, 7168], P('ep'), may hold values from -0.1875 to 0.1875
Outputs:
- mixed: bfloat16 [512, 2, 7168], P(('rep', 'ep')), parts along dimension 0
There are 2 independent parts, one for each index of `rep`. A program takes and returns all parts, laid end to end along the dimension named above; an argument that names none is the same for every part. Nothing has to cross between parts.
Inputs may be any that keep to these rules, and one draw needn't show every extreme that they name: `expert_ids`: each row names 8 different experts. In each aligned block of 4 rows (the rows of one device), the rows that name the same expert carry the distinct slots 0 up to their number minus one for it; in every block some expert is named by all 4 rows.
All inputs are finite; a program needn't handle non-finite values.
Results may differ from a plain program's by a relative error of at most 0.0065.
Values may be sent and summed in bfloat16 or wider, within the bound.
No kernel may reach another device: no remote copies, remote signals or barrier semaphores. Data moves between devices by JAX's collectives and lax.ppermute only.
A program may use at most 128 MiB of HBM per device.

v0:
```python
import functools
import math

import jax
import jax.numpy as jnp
from jax import lax
from jax.experimental import pallas as pl
from jax.experimental.pallas import tpu as pltpu
from jax.sharding import Mesh
from jax.sharding import PartitionSpec as P


D = 7168
LAT = 512
EXPERTS = 16
TOP = 8
CAP = 2
QK = 192

CORES = 2
NEAR = 4
FAR = 4
RING = NEAR * FAR
SLOTS = RING * CAP
LATE = FAR * CAP
EARLY = SLOTS - LATE
EXTRA = 128

route_scale = 2.827
norm_eps = 1e-06


ZAX = ("zb", "j")
f32, bf16 = jnp.float32, jnp.bfloat16
NT = (((1,), (1,)), ((), ()))


def swap_x(a, bits):
    return lax.ppermute(a, "x", [(i, i ^ bits) for i in range(lax.axis_size("x"))])


def shift_z(a, step):
    return lax.ppermute(a, ZAX, [(i, (i + step) % RING) for i in range(RING)])


def swap_far(a, bits):
    return lax.ppermute(a, "zb", [(i, i ^ bits) for i in range(FAR)])


def swap_core(a):
    return lax.ppermute(a, "c", [(i, i ^ 1) for i in range(CORES)])


def iota(shape, axis):
    return lax.broadcasted_iota(jnp.int32, shape, axis)


def one_hot(mask):
    return jnp.where(mask, 1.0, 0.0).astype(bf16)


COLUMNS = (0, 1, 3, 2)


def column(index, x):
    return x ^ jnp.where(index == 2, 3, jnp.where(index == 3, 2, index))


STEPS = (0, 1, RING - 1, 2, RING - 2)


def chip_at(place, where_ref):
    group, bits = place // FAR, lax.rem(place, FAR)
    step = 0
    for i, value in enumerate(STEPS):
        step = jnp.where(group == i, value, step)
    chip = lax.rem(NEAR * where_ref[1] + where_ref[2] + step, RING)
    return NEAR * ((chip // NEAR) ^ bits) + lax.rem(chip, NEAR)


def of_tile(rows, n, tiles):
    size = rows.shape[0] // len(STEPS)
    if n < tiles // 2:
        return rows[: 4 * size]
    return jnp.concatenate([rows[: 3 * size], rows[4 * size :]], axis=0)


def smem():
    return pl.BlockSpec(memory_space=pltpu.SMEM)


def vmem():
    return pl.BlockSpec(memory_space=pltpu.VMEM)


def hbm():
    return pl.BlockSpec(memory_space=pltpu.HBM)


def held_in_hbm(a):
    return pltpu.with_memory_space_constraint(a, pltpu.HBM)


def held_in_vmem(a):
    return pltpu.with_memory_space_constraint(a, pltpu.VMEM)


def params(mib):
    return pltpu.CompilerParams(vmem_limit_bytes=mib << 20)


def cost(flops, nbytes):
    return pl.CostEstimate(flops=flops, bytes_accessed=nbytes, transcendentals=0)


def context_kernel(nx, where_ref, keys, queries, new, out, held):
    seq = pl.program_id(0)
    seqs = pl.num_programs(0)
    steps, heads = queries.shape[1], queries.shape[2]
    count = steps * heads
    scale = 1.0 / math.sqrt(QK)
    query = queries[0].reshape(count, queries.shape[3])
    score = jnp.dot(query, keys[0], preferred_element_type=f32) * scale
    score = jnp.where(iota(score.shape, 1) < where_ref[3 + seq], score, -jnp.inf)
    wide = query.astype(f32)
    step_of = iota((count, 1), 0) // heads
    latest = []
    peak = jnp.max(score, axis=1, keepdims=True)
    for t in range(steps):
        key = new[0, t : t + 1, :].astype(f32)
        got = jnp.sum(wide * key, axis=1, keepdims=True) * scale
        got = jnp.where(step_of >= t, got, -jnp.inf)
        latest.append(got)
        peak = jnp.maximum(peak, got)
    probs = jnp.exp(score - peak)
    total = jnp.sum(probs, axis=1, keepdims=True)
    latest = [jnp.exp(got - peak) for got in latest]
    for got in latest:
        total = total + got
    share = 1.0 / total
    probs = (probs * share).astype(bf16)
    context = lax.dot_general(probs, keys[0, :LAT, :], NT, preferred_element_type=f32)
    for t, got in enumerate(latest):
        part = (got * share).astype(bf16).astype(f32)
        context = context + part * new[0, t : t + 1, :LAT].astype(f32)
    held[pl.ds(pl.multiple_of(seq * count, count), count), :] = context.astype(bf16)

    @pl.when(seq == seqs - 1)
    def _():
        rows = held.shape[0]
        tok = rows // heads
        shape = (rows, rows)
        to, source = iota(shape, 0), iota(shape, 1)
        hop = lax.rem(to // tok, nx)
        head = column(hop, where_ref[0]) * RING + to // (tok * nx)
        take = (lax.rem(to, tok) == source // heads) & (head == lax.rem(source, heads))
        out[...] = jnp.dot(one_hot(take), held[...], preferred_element_type=f32).astype(bf16)


def context_rows(where, nx, cache_kv, new_kv, queries):
    seqs, length, width = cache_kv.shape
    steps, heads = queries.shape[1:3]
    rows = seqs * steps * heads
    keys = jnp.swapaxes(cache_kv, 1, 2)
    return pl.pallas_call(
        functools.partial(context_kernel, nx),
        grid=(seqs,),
        out_shape=jax.ShapeDtypeStruct((rows, LAT), bf16),
        in_specs=[
            smem(),
            pl.BlockSpec((1, width, length), lambda b: (b, 0, 0)),
            pl.BlockSpec((1, steps, heads, width), lambda b: (b, 0, 0, 0)),
            pl.BlockSpec((1, steps, width), lambda b: (b, 0, 0)),
        ],
        out_specs=pl.BlockSpec((rows, LAT), lambda b: (0, 0)),
        scratch_shapes=[pltpu.VMEM((rows, LAT), bf16)],
        compiler_params=params(24),
        cost_estimate=cost(2 * rows * length * (width + LAT), 2 * cache_kv.size),
        name="context_rows",
    )(where, held_in_hbm(keys), held_in_hbm(queries), held_in_hbm(new_kv))


def pack_kernel(up, rows, tops, lows, sem):
    half, at = tops.shape[0], up.shape[1]
    copies = []
    for i, out in enumerate((tops, lows)):
        part = pl.ds(i * half, half)
        copies.append(pltpu.make_async_copy(rows.at[part], out.at[:, pl.ds(at, rows.shape[1])], sem.at[i, 0]))
        copies.append(pltpu.make_async_copy(up.at[part], out.at[:, pl.ds(0, at)], sem.at[i, 1]))
    for copy in copies:
        copy.start()
    for copy in copies:
        copy.wait()


def pack(up, rows):
    shape = (rows.shape[0] // 2, up.shape[1] + rows.shape[1])
    return pl.pallas_call(
        pack_kernel,
        out_shape=(jax.ShapeDtypeStruct(shape, bf16),) * 2,
        in_specs=[hbm()] * 2,
        out_specs=[vmem()] * 2,
        scratch_shapes=[pltpu.SemaphoreType.DMA((2, 2))],
        compiler_params=params(12),
        cost_estimate=cost(1, 4 * rows.size),
        name="pack",
    )(held_in_hbm(up), held_in_hbm(rows))


def join_kernel(count, *refs):
    at = 0
    for ref in refs[:count]:
        refs[count][pl.ds(at, ref.shape[0])] = ref[...]
        at += ref.shape[0]


def join(*arrays):
    rows, width = sum(a.shape[0] for a in arrays), arrays[0].shape[1]
    return pl.pallas_call(
        functools.partial(join_kernel, len(arrays)),
        out_shape=jax.ShapeDtypeStruct((rows, width), bf16),
        in_specs=[vmem()] * len(arrays),
        out_specs=vmem(),
        compiler_params=params(4),
        cost_estimate=cost(rows * width, 4 * rows * width),
        name="join",
    )(*arrays)


HALVES = 2
TILE = 256


def put_rows(got, outs, n):
    own, right, left, ahead, behind = outs
    size, width = own.shape[0], ahead.shape[1]
    cols = pl.ds(n * TILE, TILE)
    own[:, cols] = got[:size]
    right[:, cols] = got[size : 2 * size].astype(bf16)
    left[:, cols] = got[2 * size : 3 * size].astype(bf16)
    last, at = (ahead, n * TILE) if n * TILE < width else (behind, n * TILE - width)
    last[:, pl.ds(at, TILE)] = got[3 * size :].astype(bf16)


def row_shapes(size, width):
    return (
        jax.ShapeDtypeStruct((size, width), f32),
        jax.ShapeDtypeStruct((size, width), bf16),
        jax.ShapeDtypeStruct((size, width), bf16),
        jax.ShapeDtypeStruct((size, width // 2), bf16),
        jax.ShapeDtypeStruct((size, width // 2), bf16),
    )


def tiles_of(parts, at, n):
    half = (parts[0].shape[1] - at) // HALVES
    got = [p[:, pl.ds(at + c * half + n * TILE, TILE)] for c in range(HALVES) for p in parts]
    return jnp.concatenate(got, axis=0)


def attend_kernel(tok, nx, count, hops, last, where_ref, arrived, *refs):
    pieces, outs = refs[:count], refs[count:]
    if last:
        before, outs = outs[0], outs[1:]
    up = jnp.concatenate([piece[:, pl.ds(0, LAT)] for piece in pieces], axis=0)
    values = lax.dot_general(arrived[...], up, NT, preferred_element_type=f32)
    hop = lax.rem(iota(values.shape, 0) // tok, nx)
    part = iota(values.shape, 1) // (values.shape[1] // len(hops))
    wanted = sum(jnp.where(part == i, value, 0) for i, value in enumerate(hops))
    values = jnp.where(hop == wanted, values, 0.0).astype(bf16)
    shape = (len(STEPS) * FAR * HALVES * tok, arrived.shape[0])
    row, source = iota(shape, 0), iota(shape, 1)
    chip = chip_at(row // (HALVES * tok), where_ref)
    take = (source // (tok * nx) == chip) & (lax.rem(source, tok) == lax.rem(row, tok))
    half = lax.rem(row // tok, HALVES)
    taken = [
        jnp.dot(one_hot(take & (half == c)), values, preferred_element_type=f32).astype(bf16)
        for c in range(HALVES)
    ]
    values = jnp.concatenate(taken, axis=1)
    tiles = outs[0].shape[1] // TILE
    for n in range(tiles):
        got = jnp.dot(of_tile(values, n, tiles), tiles_of(pieces, LAT, n), preferred_element_type=f32)
        cols = pl.ds(n * TILE, TILE)
        if last:
            put_rows(before[:, cols] + got, outs, n)
        else:
            outs[0][:, cols] = got


def attend_part(where, nx, arrived, pieces, hops, tok, before):
    depth = sum(p.shape[0] for p in pieces)
    width = (pieces[0].shape[1] - LAT) // HALVES
    count = len(pieces)
    last = before is not None
    part = jax.ShapeDtypeStruct((RING * HALVES * tok, width), f32)
    return pl.pallas_call(
        functools.partial(attend_kernel, tok, nx, count, hops, last),
        out_shape=row_shapes(FAR * HALVES * tok, width) if last else part,
        in_specs=[smem(), vmem()] + [vmem()] * count + [vmem()] * last,
        out_specs=[vmem()] * 5 if last else vmem(),
        compiler_params=params(6),
        cost_estimate=cost(8 * RING * tok * depth * width * HALVES, 4 * depth * width),
        name="attend_part",
    )(where, arrived, *pieces, *([before] if last else []))


SEND_TILE = 512


def slot_rows(tok, nx, where_ref, table):
    count = table.shape[0]
    shape = (nx * CAP, EXTRA)
    row, place = iota(shape, 0), iota(shape, 1)
    expert = FAR * column(row // CAP, where_ref[0]) + where_ref[1]
    hot = one_hot(place == lax.rem(row, CAP) * EXPERTS + expert)
    got = lax.dot_general(hot, table, NT, preferred_element_type=f32)
    shape = (count // (HALVES * tok) * CAP, count)
    slot, token = iota(shape, 0), iota(shape, 1)
    same = slot // CAP == token // (HALVES * tok)
    half = lax.rem(token // tok, HALVES)
    parts = []
    for c in range(HALVES):
        for r in range(nx):
            sel = jnp.where(lax.rem(slot, CAP) == 0, got[CAP * r : CAP * r + 1], got[CAP * r + 1 : CAP * r + 2])
            parts.append(jnp.where(same & (half == c), sel, 0.0))
    return jnp.concatenate(parts, axis=0).astype(bf16)


def dispatch_kernel(tok, nx, inputs, where_ref, *refs):
    tokens, outs = refs[:inputs], refs[inputs:]
    width = tokens[0].shape[1]
    half = width - EXTRA

    def columns(at, size):
        return jnp.concatenate([ref[:, pl.ds(at, size)] for ref in tokens], axis=0)

    table = columns(half, EXTRA)
    both = slot_rows(tok, nx, where_ref, table)
    rows = both.shape[0] // HALVES
    slots = rows // nx
    for n in range(half // SEND_TILE):
        got = jnp.dot(both, columns(n * SEND_TILE, SEND_TILE), preferred_element_type=f32).astype(bf16)
        for c in range(HALVES):
            for r in range(nx):
                at = c * rows + r * slots
                outs[r][:, pl.ds(c * half + n * SEND_TILE, SEND_TILE)] = got[at : at + slots]
    got = jnp.dot(both[:rows], table, preferred_element_type=f32).astype(bf16)
    for r in range(nx):
        outs[r][:, pl.ds(HALVES * half, EXTRA)] = got[r * slots : (r + 1) * slots]


def dispatch(where, nx, tokens, tok):
    count, width = sum(a.shape[0] for a in tokens), tokens[0].shape[1]
    full = HALVES * (width - EXTRA) + EXTRA
    slots = count // (HALVES * tok) * CAP
    return pl.pallas_call(
        functools.partial(dispatch_kernel, tok, nx, len(tokens)),
        out_shape=(jax.ShapeDtypeStruct((slots, full), bf16),) * nx,
        in_specs=[smem()] + [vmem()] * len(tokens),
        out_specs=[vmem()] * nx,
        compiler_params=params(12),
        cost_estimate=cost(2 * nx * slots * count * full, 4 * count * width),
        name="dispatch",
    )(where, *tokens)


def plan_kernel(tok, nx, inputs, group, turn, where_ref, *refs):
    tokens, out = refs[:inputs], refs[inputs]
    width = tokens[0].shape[1]
    table = jnp.concatenate([ref[:, pl.ds(width - EXTRA, EXTRA)] for ref in tokens], axis=0)
    both = slot_rows(tok, nx, where_ref, table)
    shape = (out.shape[0], table.shape[0])
    row, token = iota(shape, 0), iota(shape, 1)
    unit = HALVES * tok
    wanted = chip_at(group * FAR + row // unit, where_ref)
    source = token // unit
    chip = NEAR * lax.rem(source, FAR) + lax.rem(where_ref[2] + turn + source // FAR, NEAR)
    take = (chip == wanted) & (lax.rem(token, unit) == lax.rem(row, unit))
    out[...] = lax.dot_general(one_hot(take), both, NT, preferred_element_type=f32).astype(bf16)


def plan(where, nx, tokens, tok, group, groups, turn):
    count = sum(a.shape[0] for a in tokens)
    unit = HALVES * tok
    shape = (groups * FAR * unit, HALVES * nx * (count // unit * CAP))
    return pl.pallas_call(
        functools.partial(plan_kernel, tok, nx, len(tokens), group, turn),
        out_shape=jax.ShapeDtypeStruct(shape, bf16),
        in_specs=[smem()] + [vmem()] * len(tokens),
        out_specs=vmem(),
        compiler_params=params(4),
        cost_estimate=cost(2 * shape[0] * shape[1] * count, 2 * shape[0] * shape[1]),
        name="plan",
    )(where, *tokens)


CHUNKS = 14


def pair_kernel(first, second, out, sem):
    rows = first.shape[0]
    copies = [
        pltpu.make_async_copy(ref, out.at[pl.ds(i * rows, rows)], sem.at[i])
        for i, ref in enumerate((first, second))
    ]
    for copy in copies:
        copy.start()
    for copy in copies:
        copy.wait()


def pair(first, second):
    rows, width = first.shape
    return pl.pallas_call(
        pair_kernel,
        out_shape=jax.ShapeDtypeStruct((2 * rows, width), bf16),
        in_specs=[hbm()] * 2,
        out_specs=vmem(),
        scratch_shapes=[pltpu.SemaphoreType.DMA((2,))],
        compiler_params=params(4),
        cost_estimate=cost(1, 8 * rows * width),
        name="pair",
    )(held_in_hbm(first), held_in_hbm(second))


def stage_kernel(gate, up, others, down_a, down_b, wide, deep, sem):
    rows, part = gate.shape
    parts = gate, others.at[pl.ds(0, rows)], up, others.at[pl.ds(rows, rows)]
    copies = [
        pltpu.make_async_copy(ref, wide.at[:, pl.ds(i * part, part)], sem.at[i])
        for i, ref in enumerate(parts)
    ]
    copies += [
        pltpu.make_async_copy(ref, deep.at[pl.ds(i * part, part)], sem.at[4 + i])
        for i, ref in enumerate((down_a, down_b))
    ]
    for copy in copies:
        copy.start()
    for copy in copies:
        copy.wait()


def stage(weights):
    dim, part = weights[0].shape
    return pl.pallas_call(
        stage_kernel,
        out_shape=(
            jax.ShapeDtypeStruct((dim, 4 * part), bf16),
            jax.ShapeDtypeStruct((2 * part, dim), bf16),
        ),
        in_specs=[hbm()] * 5,
        out_specs=[vmem()] * 2,
        scratch_shapes=[pltpu.SemaphoreType.DMA((6,))],
        compiler_params=params(4),
        cost_estimate=cost(4 * 1000 * dim * part, 12 * dim * part),
        name="stage",
    )(*[held_in_hbm(w) for w in weights])


def expert_kernel(groups, where_ref, *refs):
    tokens, refs = refs[: 2 * groups], refs[2 * groups :]
    (wide, deep), (early, late) = refs[:2], (refs[2 : groups + 2], refs[groups + 2 : -1])
    held = refs[-1]
    dim = wide.shape[0]
    part = wide.shape[1] // 2
    chunk = dim // CHUNKS
    chunks = CHUNKS
    for g in range(groups):
        held[pl.ds(g * SLOTS, EARLY)] = tokens[2 * g][...]
        held[pl.ds(g * SLOTS + EARLY, LATE)] = tokens[2 * g + 1][...]

    total = jnp.dot(held[:, pl.ds(0, dim)], wide[...], preferred_element_type=f32)
    gate, upward = total[:, :part], total[:, part:]
    act = (gate / (1.0 + jnp.exp(-gate)) * upward).astype(bf16)
    shape = (EXTRA, EXTRA)
    expert = FAR * where_ref[0] + where_ref[1]
    from_share = iota(shape, 0) - CAP * EXPERTS
    hot = (from_share >= 0) & (from_share < 3 * EXPERTS) & (lax.rem(from_share + EXTRA, EXPERTS) == expert)
    share = jnp.dot(held[:, pl.ds(dim, EXTRA)], one_hot(hot), preferred_element_type=f32)[:, :1]

    @pl.loop(0, 2)
    def _(i):
        for k in range(chunks // 2):
            cols = pl.ds(pl.multiple_of((i * (chunks // 2) + k) * chunk, chunk), chunk)
            got = jnp.dot(act, deep[:, cols], preferred_element_type=f32) * share
            for g in range(groups):
                rows = got[g * SLOTS : (g + 1) * SLOTS].astype(bf16)
                early[g][:, cols] = rows[:EARLY]
                late[g][:, cols] = rows[EARLY:]


def expert_part(where, tokens, weights):
    wide, deep = weights
    dim = wide.shape[0]
    groups = len(tokens) // 2
    rows = groups * SLOTS
    return pl.pallas_call(
        functools.partial(expert_kernel, groups),
        out_shape=(jax.ShapeDtypeStruct((EARLY, dim), bf16),) * groups
        + (jax.ShapeDtypeStruct((LATE, dim), bf16),) * groups,
        in_specs=[smem()] + [vmem()] * (2 * groups + 2),
        out_specs=[vmem()] * (2 * groups),
        scratch_shapes=[pltpu.VMEM((rows, dim + EXTRA), bf16)],
        compiler_params=params(8),
        cost_estimate=cost(6 * rows * wide.size, 2 * rows * dim),
        name="expert_part",
    )(where, *tokens, held_in_vmem(wide), held_in_vmem(deep))


def collect_kernel(count, spread, *refs):
    parts, (right, left, ahead, behind) = refs[:count], refs[count:]
    size = right.shape[0]
    tiles = right.shape[1] // TILE
    for n in range(tiles):
        cols = pl.ds(n * TILE, TILE)
        rows = spread[...]
        first = n < tiles // 2
        rows = rows[: 3 * size] if first else jnp.concatenate([rows[: 2 * size], rows[3 * size :]], axis=0)
        got = jnp.dot(rows, tiles_of(parts, 0, n), preferred_element_type=f32).astype(bf16)
        right[:, cols] = got[:size]
        left[:, cols] = got[size : 2 * size]
        last, at = (ahead, n * TILE) if first else (behind, (n - tiles // 2) * TILE)
        last[:, pl.ds(at, TILE)] = got[2 * size :]


def collect(spread, parts):
    width = parts[0].shape[1] // HALVES
    count = len(parts)
    return pl.pallas_call(
        functools.partial(collect_kernel, count),
        out_shape=row_shapes(spread.shape[0] // (len(STEPS) - 1), width)[1:],
        in_specs=[vmem()] * (count + 1),
        out_specs=[vmem()] * 4,
        compiler_params=params(12),
        cost_estimate=cost(2 * spread.size * width, 4 * spread.shape[0] * width),
        name="collect",
    )(spread, *parts)


def merge_kernel(count, *refs):
    mine, (right, left, ahead, behind, first), rest = refs[:count], refs[count : count + 5], refs[count + 5 :]
    block = first.shape[0]
    tiles = first.shape[1] // TILE
    for n in range(tiles):
        cols = pl.ds(n * TILE, TILE)
        if count == 1:
            total = mine[0][:, cols]
        else:
            total = jnp.dot(mine[0][...], tiles_of(mine[1:], 0, n), preferred_element_type=f32)
        last, at = (ahead, n * TILE) if n < tiles // 2 else (behind, (n - tiles // 2) * TILE)
        total = total + right[:, cols].astype(f32) + left[:, cols].astype(f32)
        total = total + last[:, pl.ds(at, TILE)].astype(f32)
        first[:, cols] = total[:block]
        for k, out in enumerate(rest):
            out[:, cols] = total[(k + 1) * block : (k + 2) * block].astype(bf16)


def merge(mine, others):
    size, width = others[0].shape
    block = (size // FAR, width)
    return pl.pallas_call(
        functools.partial(merge_kernel, len(mine)),
        out_shape=(jax.ShapeDtypeStruct(block, f32),) + (jax.ShapeDtypeStruct(block, bf16),) * (FAR - 1),
        in_specs=[vmem()] * (len(mine) + 4),
        out_specs=[vmem()] * FAR,
        compiler_params=params(4),
        cost_estimate=cost(4 * size * width, 12 * size * width),
        name="merge",
    )(*mine, *others)


def half_swap(a):
    middle = a.shape[0] // 2
    return jnp.concatenate([a[middle:], a[:middle]], axis=0)


def route_kernel(first, one, two, three, rows, gain, router, ids, slots, hidden, payload):
    count, half = rows.shape
    total = first[...] + one[...].astype(f32) + two[...].astype(f32) + three[...].astype(f32)
    total = rows[...].astype(f32) + total
    hidden[...] = total
    square = jnp.sum(total * total, axis=1, keepdims=True)
    scale = lax.rsqrt((square + half_swap(square)) / D + norm_eps)
    normed = (total * scale * gain[...]).astype(bf16)
    payload[:, pl.ds(0, half)] = normed
    parts = [
        lax.dot_general(normed, router[:, pl.ds(c * half, half)], NT, preferred_element_type=f32)
        for c in range(HALVES)
    ]
    logits = jnp.where(iota(parts[0].shape, 0) < count // 2, parts[0], parts[1])
    logits = logits + half_swap(logits)
    logits = jnp.concatenate([logits] * (EXTRA // EXPERTS), axis=1)
    lane = iota(logits.shape, 1)
    place = jnp.zeros(logits.shape, jnp.int32)
    for k in range(TOP):
        place = jnp.where(lax.rem(lane, EXPERTS) == ids[:, k : k + 1], slots[:, k : k + 1] + 1, place)
    gates = jnp.where(place > 0, 1.0 / (1.0 + jnp.exp(-logits)), 0.0)
    share = route_scale * gates / jnp.sum(jnp.where(lane < EXPERTS, gates, 0.0), axis=1, keepdims=True)
    kind = lane // EXPERTS
    table = jnp.zeros(logits.shape, f32)
    for n in range(CAP):
        table = jnp.where((kind == n) & (place == n + 1), 1.0, table)
    rest = share
    for n in range(3):
        piece = rest.astype(bf16).astype(f32)
        table = jnp.where(kind == CAP + n, piece, table)
        rest = rest - piece
    payload[:, pl.ds(half, EXTRA)] = table.astype(bf16)


def route(added, rows, gain, router, ids, slots):
    count, half = rows.shape
    return pl.pallas_call(
        route_kernel,
        out_shape=(
            jax.ShapeDtypeStruct((count, half), f32),
            jax.ShapeDtypeStruct((count, half + EXTRA), bf16),
        ),
        in_specs=[vmem()] * 9,
        out_specs=[vmem()] * 2,
        compiler_params=params(4),
        cost_estimate=cost(4 * count * half * EXPERTS, 20 * count * half),
        name="route",
    )(*added, rows, gain, router, ids, slots)


def finish_kernel(hidden, first, one, two, three, out):
    seqs, steps, _ = out.shape
    half = hidden.shape[1]
    total = first[...] + one[...].astype(f32) + two[...].astype(f32) + three[...].astype(f32)
    total = (hidden[...] + total).astype(bf16)
    for c in range(HALVES):
        for b in range(seqs):
            at = (c * seqs + b) * steps
            out[b, :, pl.ds(c * half, half)] = total[at : at + steps]


def finish(hidden, added, shape):
    return pl.pallas_call(
        finish_kernel,
        out_shape=jax.ShapeDtypeStruct(shape, bf16),
        in_specs=[vmem()] * 5,
        out_specs=vmem(),
        compiler_params=params(4),
        cost_estimate=cost(5 * hidden.size, 14 * hidden.size),
        name="finish",
    )(hidden, *added)


def reduce_z(mine, right, left, ahead, behind):
    others = shift_z(right, 1), shift_z(left, -1), shift_z(ahead, 2), shift_z(behind, -2)
    first, *sent = merge(mine, others)
    others = [swap_far(rows, k + 1) for k, rows in enumerate(sent)]
    return first, *others


def layer(
    cache_kv,
    new_kv,
    queries,
    lengths,
    resid,
    value_up,
    out_proj,
    norm_gain,
    router,
    expert_ids,
    slots,
    w_gate,
    w_up,
    w_down,
):
    nx = lax.axis_size("x")
    seqs, steps = queries.shape[:2]
    tok = seqs * steps
    where = jnp.stack([lax.axis_index(a) for a in ("x", "zb", "j")]).astype(jnp.int32)
    where = jnp.concatenate([where, lengths.astype(jnp.int32)])

    tops, lows = pack(value_up.T, out_proj)
    top_left = swap_x(tops, 1)
    low_right = swap_x(lows, 3)
    low_left = swap_x(lows, 1)
    top_right = swap_x(tops, 3)

    outgoing = context_rows(where, nx, cache_kv, new_kv, queries)
    arrived = lax.all_to_all(
        outgoing.reshape(RING, nx * tok, LAT), ZAX, split_axis=0, concat_axis=0, tiled=True
    )
    top_far = swap_x(top_left, 3)
    low_far = swap_x(low_right, 1)
    mine = join(tops, lows)
    near = join(top_left, low_left, top_right, low_right)
    pieces = [mine, swap_core(mine)]
    pieces += [near, swap_core(near)]
    beyond = [top_far, low_far, swap_core(top_far), swap_core(low_far)]
    both = pair(w_gate, w_up)
    others = swap_core(both), swap_core(w_down)
    weights = stage((w_gate, w_up, others[0], w_down, others[1]))
    arrived = arrived.reshape(RING * nx * tok, LAT)
    most = attend_part(where, nx, arrived, pieces, (0, 0, 1, 2, 1, 2), tok, None)
    own, *rows = attend_part(where, nx, arrived, beyond, (3,) * 4, tok, most)
    added = reduce_z((own,), *rows)

    half = D // HALVES
    rows = resid.reshape(tok, HALVES, half).swapaxes(0, 1).reshape(HALVES * tok, half)
    gain = jnp.repeat(norm_gain.astype(f32).reshape(HALVES, half), tok, axis=0)
    ids, places = [
        jnp.tile(a.reshape(tok, TOP).astype(jnp.int32), (HALVES, 1)) for a in (expert_ids, slots)
    ]
    hidden, payload = route(added, rows, gain, router.T, ids, places)

    ring = lax.all_gather(payload, "zb", axis=0, tiled=True)
    middle = ring.shape[0] // 2
    above, below = shift_z(ring, -1), shift_z(ring, 1)
    beyond = shift_z(ring[:middle], -2), shift_z(ring[middle:], 2)
    near = (above, *beyond, below)
    sent = dispatch(where, nx, (ring,), tok)
    late_in = [swap_x(sent[i], COLUMNS[i]) for i in range(1, nx)]
    late_in = [sent[0], *late_in]
    sent = dispatch(where, nx, near, tok)
    early_in = [swap_x(sent[i], COLUMNS[i]) for i in range(1, nx)]
    early_in = [sent[0], *early_in]
    late = plan(where, nx, (ring,), tok, 0, 1, 0)
    early = plan(where, nx, near, tok, 1, len(STEPS) - 1, 1)
    got = [pair for pairs in zip(early_in, late_in) for pair in pairs]
    first = expert_part(where, got[2:6], weights)
    second = expert_part(where, got[:2] + got[6:], weights)
    done = [[second[2 * n], *first[2 * n : 2 * n + 2], second[2 * n + 1]] for n in range(2)]
    first = [done[0][0]] + [swap_x(done[0][i], COLUMNS[i]) for i in range(1, nx)]
    second = [done[1][0]] + [swap_x(done[1][i], COLUMNS[i]) for i in range(1, nx)]
    added = reduce_z((late, *second), *collect(early, first))
    return finish(hidden, added, resid.shape)


def solution(mesh):
    chips = mesh.shape["ep"] // (RING * CORES)
    grid = mesh.devices.reshape(mesh.shape["rep"], chips, FAR, NEAR, CORES)
    fine = Mesh(grid, ("rep", "x", "zb", "j", "c"))
    ep = ("x", "zb", "j", "c")
    both = ("rep",) + ep
    return jax.shard_map(
        layer,
        mesh=fine,
        in_specs=(
            P(both, None, None),
            P(both, None, None),
            P(both, None, None, None),
            P(both),
            P(both, None, None),
            P(None, ep),
            P(ep, None),
            P(),
            P(),
            P(both, None, None),
            P(both, None, None),
            P(None, ep),
            P(None, ep),
            P(ep, None),
        ),
        out_specs=P(both, None, None),
        check_vma=False,
    )
```

profile of v0, /device:TPU:426, one launch (start us, length us, event | category | flops | bytes accessed | tf_op | source)
XLA Modules:
  0.0 237.5 jit_solution(14308979612388854339)
XLA Ops:
  0.0 1.2 pack.1
  1.2 1.7 collective-permute-start.8
  3.0 1.9 collective-permute-start
  5.4 10.0 %collective-permute-done.8.refs_2_ = bf16[32,7680]{1,0:T(8,128)(2,1)S(1)} collective-permute-done((bf16[32,7680]{1,0:T(8,128)(2,1)S(1)}, bf16[32,7680]{1,0:T(8,128)(2,1)S(1)}, u32[]{:S(2)}, u32[]{:S(2)}) %collective-permute-start.8) | collective-permute-done | bytes 491552 | tf_op jit(solution)/shard_map/ppermute | solution.py:39
  15.4 1.6 collective-permute-done.refs_0_
  17.1 9.4 %collective-permute-done.7.refs_1_ = bf16[32,7680]{1,0:T(8,128)(2,1)S(1)} collective-permute-done((bf16[32,7680]{1,0:T(8,128)(2,1)S(1)}, bf16[32,7680]{1,0:T(8,128)(2,1)S(1)}, u32[]{:S(2)}, u32[]{:S(2)}) %collective-permute-start.7) | collective-permute-done | bytes 491552 | tf_op jit(solution)/shard_map/ppermute | solution.py:39
  26.6 0.7 copy-done.1
  27.3 3.9 %pair.1 = bf16[14336,128]{1,0:T(8,128)(2,1)} custom-call(bf16[7168,128]{1,0:T(8,128)(2,1)} %gate.1, bf16[7168,128]{1,0:T(8,128)(2,1)} %up.1), custom_call_target="tpu_custom_call" | custom-call | flops 1 | bytes 7340032 | tf_op jit(solution)/shard_map/pair/pallas_call | solution.py:415
  31.1 0.6 collective-permute-start.23
  32.1 5.9 %context_rows.1 = bf16[256,512]{1,0:T(8,128)(2,1)} custom-call(s32[5]{0:T(128)S(1)} %pad_add_fusion.where_ref, bf16[2,576,2048]{2,1,0:T(8,128)(2,1)} %bitcast.20, bf16[2,2,64,576]{3,2,1,0:T(8,128)(2,1)} %queries.1, bf16[2,2,576]{2,1,0:T(2,128)(2,1)} %new.1), custom_call_target="tpu_custom_call" | custom-call | flops 1140850688 | bytes 4718592 | tf_op jit(solution)/shard_map/context_rows/pallas_call | solution.py:165
  38.0 20.3 %all-to-all-start = ((bf16[16,16,512]{2,1,0:T(8,128)(2,1)}), bf16[16,16,512]{2,1,0:T(8,128)(2,1)S(1)}, u32[]{:S(2)}, u32[]{:S(2)}) async-start(bf16[16,16,512]{2,1,0:T(8,128)(2,1)} %bitcast.4), calls=%async_computation | async-start | bytes 524288 | tf_op jit(solution)/shard_map/all_to_all | solution.py:687
  58.5 3.0 %collective-permute-start.3 = (bf16[32,7680]{1,0:T(8,128)(2,1)}, bf16[32,7680]{1,0:T(8,128)(2,1)}, u32[]{:S(2)}, u32[]{:S(2)}) collective-permute-start(bf16[32,7680]{1,0:T(8,128)(2,1)} %copy-done.1), channel_id=1, source_target_pairs={{0,32},{32,0},{64,96},{96,64},{1,33},{33,1},{65,97},{97,65},{2,34}... | collective-permute-start | bytes 1474568 | tf_op jit(solution)/shard_map/ppermute | solution.py:39
  61.5 10.1 %collective-permute-done.1.refs_0_ = bf16[32,7680]{1,0:T(8,128)(2,1)} collective-permute-done((bf16[32,7680]{1,0:T(8,128)(2,1)}, bf16[32,7680]{1,0:T(8,128)(2,1)}, u32[]{:S(2)}, u32[]{:S(2)}) %collective-permute-start.1) | collective-permute-done | bytes 491552 | tf_op jit(solution)/shard_map/ppermute | solution.py:39
  71.6 1.2 collective-permute-done.3.refs_1_
  72.8 0.5 collective-permute-start.24
  73.3 3.5 %all-to-all-done = bf16[16,16,512]{2,1,0:T(8,128)(2,1)S(1)} async-done(((bf16[16,16,512]{2,1,0:T(8,128)(2,1)}), bf16[16,16,512]{2,1,0:T(8,128)(2,1)S(1)}, u32[]{:S(2)}, u32[]{:S(2)}) %all-to-all-start) | async-done | bytes 262176 | tf_op jit(solution)/shard_map/all_to_all | solution.py:687
  76.8 3.3 %attend_part.2.refs_4_ = f32[128,3584]{1,0:T(8,128)S(1)} custom-call(s32[5]{0:T(128)S(1)} %pad_add_fusion.where_ref, bf16[256,512]{1,0:T(8,128)(2,1)S(1)} %bitcast.15, bf16[64,7680]{1,0:T(8,128)(2,1)S(1)} %join.2.refs_0_, bf16[64,7680]{1,0:T(8,128)(2,1)} %collective-permute-done.6.refs_1_, bf16[128,7680]{1,0:T(8,128)(2,1)S(1)} %join.3.refs_2_, ...), custom_call_target="tpu_custom_call" | custom-call | flops 1409286144 | bytes 5505024 | tf_op jit(solution)/shard_map/attend_part/pallas_call | solution.py:297
  80.2 2.4 %attend_part.3 = (f32[32,3584]{1,0:T(8,128)S(1)}, bf16[32,3584]{1,0:T(8,128)(2,1)S(1)}, bf16[32,3584]{1,0:T(8,128)(2,1)S(1)}, bf16[32,1792]{1,0:T(8,128)(2,1)S(1)}, bf16[32,1792]{1,0:T(8,128)(2,1)S(1)}) custom-call(s32[5]{0:T(128)S(1)} %pad_add_fusion.where_ref, bf16[256,512]{1,0:T(8,128)(2,1)S(1)} %bitcast.16, ...), custom_call_target="tpu_custom_call" | custom-call | flops 469762048 | bytes 1835008 | tf_op jit(solution)/shard_map/attend_part/pallas_call | solution.py:297
  82.6 1.6 collective-permute-start.12
  84.7 1.6 collective-permute-start.11
  86.2 3.4 %collective-permute-done.12.refs_3_ = bf16[32,1792]{1,0:T(8,128)(2,1)S(1)} collective-permute-done((bf16[32,1792]{1,0:T(8,128)(2,1)S(1)}, bf16[32,1792]{1,0:T(8,128)(2,1)S(1)}, u32[]{:S(2)}, u32[]{:S(2)}) %collective-permute-start.12) | collective-permute-done | bytes 114720 | tf_op jit(solution)/shard_map/ppermute | solution.py:43
  89.7 2.9 %collective-permute-start.13 = (bf16[32,1792]{1,0:T(8,128)(2,1)S(1)}, bf16[32,1792]{1,0:T(8,128)(2,1)S(1)}, u32[]{:S(2)}, u32[]{:S(2)}) collective-permute-start(bf16[32,1792]{1,0:T(8,128)(2,1)S(1)} %get-tuple-element.50), channel_id=1, source_target_pairs={{0,28},{2,30},{4,0},{6,2},{8,4},{10,6},{12,8},{14,10},{16,12},{18,... | collective-permute-start | bytes 344072 | tf_op jit(solution)/shard_map/ppermute | solution.py:43
  92.6 4.1 %collective-permute-done.13.refs_4_ = bf16[32,1792]{1,0:T(8,128)(2,1)S(1)} collective-permute-done((bf16[32,1792]{1,0:T(8,128)(2,1)S(1)}, bf16[32,1792]{1,0:T(8,128)(2,1)S(1)}, u32[]{:S(2)}, u32[]{:S(2)}) %collective-permute-start.13) | collective-permute-done | bytes 114720 | tf_op jit(solution)/shard_map/ppermute | solution.py:43
  96.9 5.5 %collective-permute-start.14 = (bf16[8,3584]{1,0:T(8,128)(2,1)S(1)}, bf16[8,3584]{1,0:T(8,128)(2,1)S(1)}, u32[]{:S(2)}, u32[]{:S(2)}) collective-permute-start(bf16[8,3584]{1,0:T(8,128)(2,1)S(1)} %get-tuple-element.52), channel_id=1, source_target_pairs={{0,8},{8,0},{16,24},{24,16},{1,9},{9,1},{17,25},{25,17},{2,10},{10... | collective-permute-start | bytes 172040 | tf_op jit(solution)/shard_map/ppermute | solution.py:47
  102.3 4.3 %collective-permute-start.15 = (bf16[8,3584]{1,0:T(8,128)(2,1)S(1)}, bf16[8,3584]{1,0:T(8,128)(2,1)S(1)}, u32[]{:S(2)}, u32[]{:S(2)}) collective-permute-start(bf16[8,3584]{1,0:T(8,128)(2,1)S(1)} %get-tuple-element.53), channel_id=1, source_target_pairs={{0,16},{8,24},{16,0},{24,8},{1,17},{9,25},{17,1},{25,9},{2,18},{10... | collective-permute-start | bytes 172040 | tf_op jit(solution)/shard_map/ppermute | solution.py:47
  106.7 1.6 collective-permute-start.16
  108.5 7.9 %collective-permute-done.15.two = bf16[8,3584]{1,0:T(8,128)(2,1)S(1)} collective-permute-done((bf16[8,3584]{1,0:T(8,128)(2,1)S(1)}, bf16[8,3584]{1,0:T(8,128)(2,1)S(1)}, u32[]{:S(2)}, u32[]{:S(2)}) %collective-permute-start.15) | collective-permute-done | bytes 57376 | tf_op jit(solution)/shard_map/ppermute | solution.py:47
  116.4 0.6 route.1
  117.1 22.6 %all_gather.3.refs_0_ = bf16[32,3712]{1,0:T(8,128)(2,1)S(1)} all-gather(bf16[8,3712]{1,0:T(8,128)(2,1)S(1)} %get-tuple-element.56), channel_id=1, replica_groups=mesh['rep'=2,'x'=4,'zb'=4,'j'=4,'c'=2] {'zb'}, dimensions={0}, use_global_device_ids=true | all-gather | bytes 296960 | tf_op jit(solution)/shard_map/all_gather | solution.py:713
  139.8 1.6 collective-permute-start.20
  141.3 0.6 collective-permute-start.17
  141.9 4.0 %collective-permute-done.19.refs_2_ = bf16[16,3712]{1,0:T(8,128)(2,1)S(1)} collective-permute-done((bf16[16,3712]{1,0:T(8,128)(2,1)S(1)}, bf16[16,3712]{1,0:T(8,128)(2,1)S(1)}, u32[]{:S(2)}, u32[]{:S(2)}) %collective-permute-start.19) | collective-permute-done | bytes 118816 | tf_op jit(solution)/shard_map/ppermute | solution.py:43
  145.9 7.1 %collective-permute-done.18.refs_1_ = bf16[16,3712]{1,0:T(8,128)(2,1)S(1)} collective-permute-done((bf16[16,3712]{1,0:T(8,128)(2,1)S(1)}, bf16[16,3712]{1,0:T(8,128)(2,1)S(1)}, u32[]{:S(2)}, u32[]{:S(2)}) %collective-permute-start.18) | collective-permute-done | bytes 118816 | tf_op jit(solution)/shard_map/ppermute | solution.py:43
  153.0 1.2 dispatch.2
  154.2 4.8 %collective-permute-start.25 = (bf16[24,7296]{1,0:T(8,128)(2,1)S(1)}, bf16[24,7296]{1,0:T(8,128)(2,1)S(1)}, u32[]{:S(2)}, u32[]{:S(2)}) collective-permute-start(bf16[24,7296]{1,0:T(8,128)(2,1)S(1)} %get-tuple-element.64), channel_id=1, source_target_pairs={{0,32},{32,0},{64,96},{96,64},{1,33},{33,1},{65,97},{97,65},{2,34}... | collective-permute-start | bytes 1050632 | tf_op jit(solution)/shard_map/ppermute | solution.py:39
  159.0 0.7 collective-permute-start.27
  159.7 0.9 dispatch.3
  160.6 0.9 collective-permute-start.26
  161.5 1.3 collective-permute-start.28
  162.8 2.0 collective-permute-start.21
  164.9 4.2 %stage.1 = (bf16[7168,512]{1,0:T(8,128)(2,1)S(1)}, bf16[256,7168]{1,0:T(8,128)(2,1)S(1)}) custom-call(bf16[7168,128]{1,0:T(8,128)(2,1)} %gate.1, bf16[7168,128]{1,0:T(8,128)(2,1)} %up.1, bf16[14336,128]{1,0:T(8,128)(2,1)} %collective-permute-done.23.others, bf16[128,7168]{1,0:T(8,128)(2,1)} %down_a.1, bf16[128,7168]{1,0:T(8,128)(2,1)} %collective-permute-done.24.down_b), custom_call_target="tpu_custom_call" | custom-call | flops 3670016000 | bytes 11010048 | tf_op jit(solution)/shard_map/stage/pallas_call | solution.py:446
  169.1 0.5 collective-permute-done.26.refs_1_
  169.7 2.8 %collective-permute-start.22 = (bf16[8,7296]{1,0:T(8,128)(2,1)S(1)}, bf16[8,7296]{1,0:T(8,128)(2,1)S(1)}, u32[]{:S(2)}, u32[]{:S(2)}) collective-permute-start(bf16[8,7296]{1,0:T(8,128)(2,1)S(1)} %get-tuple-element.60), channel_id=1, source_target_pairs={{0,64},{32,96},{64,0},{96,32},{1,65},{33,97},{65,1},{97,33},{2,66}... | collective-permute-start | bytes 350216 | tf_op jit(solution)/shard_map/ppermute | solution.py:39
  172.4 1.6 collective-permute-done.28.refs_3_
  174.1 2.8 %expert_part.3 = (bf16[24,7168]{1,0:T(8,128)(2,1)S(1)}, bf16[24,7168]{1,0:T(8,128)(2,1)S(1)}, bf16[8,7168]{1,0:T(8,128)(2,1)S(1)}, bf16[8,7168]{1,0:T(8,128)(2,1)S(1)}) custom-call(s32[5]{0:T(128)S(1)} %pad_add_fusion.where_ref, bf16[24,7296]{1,0:T(8,128)(2,1)S(1)} %collective-permute-done.25.refs_0_, bf16[8,7296]{1,0:T(8,128)(2,1)S(1)} %collective-permute-done.26.refs_1_, ...), custom_call_target="tpu_custom_call" | custom-call | flops 1409286144 | bytes 917504 | tf_op jit(solution)/shard_map/expert_part/pallas_call | solution.py:498
  177.2 3.5 %collective-permute-done.22.refs_3_ = bf16[8,7296]{1,0:T(8,128)(2,1)S(1)} collective-permute-done((bf16[8,7296]{1,0:T(8,128)(2,1)S(1)}, bf16[8,7296]{1,0:T(8,128)(2,1)S(1)}, u32[]{:S(2)}, u32[]{:S(2)}) %collective-permute-start.22) | collective-permute-done | bytes 116768 | tf_op jit(solution)/shard_map/ppermute | solution.py:39
  180.7 2.8 %expert_part.2 = (bf16[24,7168]{1,0:T(8,128)(2,1)S(1)}, bf16[24,7168]{1,0:T(8,128)(2,1)S(1)}, bf16[8,7168]{1,0:T(8,128)(2,1)S(1)}, bf16[8,7168]{1,0:T(8,128)(2,1)S(1)}) custom-call(s32[5]{0:T(128)S(1)} %pad_add_fusion.where_ref, bf16[24,7296]{1,0:T(8,128)(2,1)S(1)} %get-tuple-element.57.refs_0_, bf16[8,7296]{1,0:T(8,128)(2,1)S(1)} %get-tuple-element.58.refs_1_, ...), custom_call_target="tpu_custom_call" | custom-call | flops 1409286144 | bytes 917504 | tf_op jit(solution)/shard_map/expert_part/pallas_call | solution.py:498
  183.6 2.0 collective-permute-start.34
  185.5 0.9 plan.3.spread
  186.4 0.7 collective-permute-start.29
  187.1 1.7 collective-permute-start.30
  188.8 5.1 %collective-permute-done.33.refs_2_ = bf16[24,7168]{1,0:T(8,128)(2,1)S(1)} collective-permute-done((bf16[24,7168]{1,0:T(8,128)(2,1)S(1)}, bf16[24,7168]{1,0:T(8,128)(2,1)S(1)}, u32[]{:S(2)}, u32[]{:S(2)}) %collective-permute-start.33) | collective-permute-done | bytes 344096 | tf_op jit(solution)/shard_map/ppermute | solution.py:39
  194.2 1.9 collective-permute-start.35
  196.4 3.2 %collective-permute-start.31 = (bf16[8,7168]{1,0:T(8,128)(2,1)S(1)}, bf16[8,7168]{1,0:T(8,128)(2,1)S(1)}, u32[]{:S(2)}, u32[]{:S(2)}) collective-permute-start(bf16[8,7168]{1,0:T(8,128)(2,1)S(1)} %get-tuple-element.70), channel_id=1, source_target_pairs={{0,64},{32,96},{64,0},{96,32},{1,65},{33,97},{65,1},{97,33},{2,66}... | collective-permute-start | bytes 344072 | tf_op jit(solution)/shard_map/ppermute | solution.py:39
  199.6 6.5 %collective-permute-start.37 = (bf16[32,1792]{1,0:T(8,128)(2,1)S(1)}, bf16[32,1792]{1,0:T(8,128)(2,1)S(1)}, u32[]{:S(2)}, u32[]{:S(2)}) collective-permute-start(bf16[32,1792]{1,0:T(8,128)(2,1)S(1)} %get-tuple-element.77), channel_id=1, source_target_pairs={{0,4},{2,6},{4,8},{6,10},{8,12},{10,14},{12,16},{14,18},{16,20},{1... | collective-permute-start | bytes 344072 | tf_op jit(solution)/shard_map/ppermute | solution.py:43
  206.1 1.0 collective-permute-start.38
  207.0 0.8 plan.2.refs_0_
  207.8 3.2 %collective-permute-done.37.refs_7_ = bf16[32,1792]{1,0:T(8,128)(2,1)S(1)} collective-permute-done((bf16[32,1792]{1,0:T(8,128)(2,1)S(1)}, bf16[32,1792]{1,0:T(8,128)(2,1)S(1)}, u32[]{:S(2)}, u32[]{:S(2)}) %collective-permute-start.37) | collective-permute-done | bytes 114720 | tf_op jit(solution)/shard_map/ppermute | solution.py:43
  211.0 4.2 %collective-permute-done.38.refs_8_ = bf16[32,1792]{1,0:T(8,128)(2,1)S(1)} collective-permute-done((bf16[32,1792]{1,0:T(8,128)(2,1)S(1)}, bf16[32,1792]{1,0:T(8,128)(2,1)S(1)}, u32[]{:S(2)}, u32[]{:S(2)}) %collective-permute-start.38) | collective-permute-done | bytes 114720 | tf_op jit(solution)/shard_map/ppermute | solution.py:43
  215.4 2.9 %collective-permute-start.39 = (bf16[8,3584]{1,0:T(8,128)(2,1)S(1)}, bf16[8,3584]{1,0:T(8,128)(2,1)S(1)}, u32[]{:S(2)}, u32[]{:S(2)}) collective-permute-start(bf16[8,3584]{1,0:T(8,128)(2,1)S(1)} %get-tuple-element.80), channel_id=1, source_target_pairs={{0,8},{8,0},{16,24},{24,16},{1,9},{9,1},{17,25},{25,17},{2,10},{10... | collective-permute-start | bytes 172040 | tf_op jit(solution)/shard_map/ppermute | solution.py:47
  218.4 10.4 %collective-permute-start.40 = (bf16[8,3584]{1,0:T(8,128)(2,1)S(1)}, bf16[8,3584]{1,0:T(8,128)(2,1)S(1)}, u32[]{:S(2)}, u32[]{:S(2)}) collective-permute-start(bf16[8,3584]{1,0:T(8,128)(2,1)S(1)} %get-tuple-element.81), channel_id=1, source_target_pairs={{0,16},{8,24},{16,0},{24,8},{1,17},{9,25},{17,1},{25,9},{2,18},{10... | collective-permute-start | bytes 172040 | tf_op jit(solution)/shard_map/ppermute | solution.py:47
  228.7 2.6 %collective-permute-done.40.two = bf16[8,3584]{1,0:T(8,128)(2,1)S(1)} collective-permute-done((bf16[8,3584]{1,0:T(8,128)(2,1)S(1)}, bf16[8,3584]{1,0:T(8,128)(2,1)S(1)}, u32[]{:S(2)}, u32[]{:S(2)}) %collective-permute-start.40) | collective-permute-done | bytes 57376 | tf_op jit(solution)/shard_map/ppermute | solution.py:47
  231.4 5.4 %collective-permute-done.41.three = bf16[8,3584]{1,0:T(8,128)(2,1)S(1)} collective-permute-done((bf16[8,3584]{1,0:T(8,128)(2,1)S(1)}, bf16[8,3584]{1,0:T(8,128)(2,1)S(1)}, u32[]{:S(2)}, u32[]{:S(2)}) %collective-permute-start.41) | collective-permute-done | bytes 57376 | tf_op jit(solution)/shard_map/ppermute | solution.py:47
  236.8 0.7 finish.1
  (68 shorter events, 3.3 us)
Async XLA Ops:
  1.2 14.2 %collective-permute-start.8 = (bf16[32,7680]{1,0:T(8,128)(2,1)S(1)}, bf16[32,7680]{1,0:T(8,128)(2,1)S(1)}, u32[]{:S(2)}, u32[]{:S(2)}) collective-permute-start(bf16[32,7680]{1,0:T(8,128)(2,1)S(1)} %get-tuple-element.44.refs_0_), channel_id=1, source_target_pairs={{0,96},{32,64},{64,32},{96,0},{1,97},{33,65},{65,33},{97,1},{2,98}... | collective-permute-start | bytes 1474568 | tf_op jit(solution)/shard_map/ppermute | solution.py:39
  3.0 14.1 %collective-permute-start = (bf16[32,7680]{1,0:T(8,128)(2,1)S(1)}, bf16[32,7680]{1,0:T(8,128)(2,1)S(1)}, u32[]{:S(2)}, u32[]{:S(2)}) collective-permute-start(bf16[32,7680]{1,0:T(8,128)(2,1)S(1)} %get-tuple-element.44.refs_0_), channel_id=1, source_target_pairs={{0,32},{32,0},{64,96},{96,64},{1,33},{33,1},{65,97},{97,65},{2,34}... | collective-permute-start | bytes 1474568 | tf_op jit(solution)/shard_map/ppermute | solution.py:39
  4.9 21.5 %collective-permute-start.7 = (bf16[32,7680]{1,0:T(8,128)(2,1)S(1)}, bf16[32,7680]{1,0:T(8,128)(2,1)S(1)}, u32[]{:S(2)}, u32[]{:S(2)}) collective-permute-start(bf16[32,7680]{1,0:T(8,128)(2,1)S(1)} %get-tuple-element.45.refs_1_), channel_id=1, source_target_pairs={{0,32},{32,0},{64,96},{96,64},{1,33},{33,1},{65,97},{97,65},{2,34}... | collective-permute-start | bytes 1474568 | tf_op jit(solution)/shard_map/ppermute | solution.py:39
  5.0 21.5 %collective-permute-start.2 = (bf16[32,7680]{1,0:T(8,128)(2,1)S(1)}, bf16[32,7680]{1,0:T(8,128)(2,1)S(1)}, u32[]{:S(2)}, u32[]{:S(2)}) collective-permute-start(bf16[32,7680]{1,0:T(8,128)(2,1)S(1)} %get-tuple-element.45.refs_1_), channel_id=1, source_target_pairs={{0,96},{32,64},{64,32},{96,0},{1,97},{33,65},{65,33},{97,1},{2,98}... | collective-permute-start | bytes 1474568 | tf_op jit(solution)/shard_map/ppermute | solution.py:39
  17.1 9.5 %copy-start = (bf16[32,7680]{1,0:T(8,128)(2,1)}, bf16[32,7680]{1,0:T(8,128)(2,1)S(1)}, u32[]{:S(2)}) copy-start(bf16[32,7680]{1,0:T(8,128)(2,1)S(1)} %collective-permute-done.refs_0_) | copy-start | bytes 1474564
  26.4 0.8 copy-start.1
  27.3 49.6 %collective-permute-start.9 = (bf16[128,7680]{1,0:T(8,128)(2,1)S(1)}, bf16[128,7680]{1,0:T(8,128)(2,1)}, u32[]{:S(2)}, u32[]{:S(2)}) collective-permute-start(bf16[128,7680]{1,0:T(8,128)(2,1)S(1)} %join.3.refs_2_), channel_id=1, source_target_pairs={{0,1},{1,0},{2,3},{3,2},{4,5},{5,4},{6,7},{7,6},{8,9},{9,8},{10,11... | collective-permute-start | bytes 5898248 | tf_op jit(solution)/shard_map/ppermute | solution.py:51
  31.1 0.9 copy-start.7
  31.1 131.7 %collective-permute-start.23 = (bf16[14336,128]{1,0:T(8,128)(2,1)}, bf16[14336,128]{1,0:T(8,128)(2,1)}, u32[]{:S(2)}, u32[]{:S(2)}) collective-permute-start(bf16[14336,128]{1,0:T(8,128)(2,1)} %pair.1), channel_id=1, source_target_pairs={{0,1},{1,0},{2,3},{3,2},{4,5},{5,4},{6,7},{7,6},{8,9},{9,8},{10,11... | collective-permute-start | bytes 11010056 | tf_op jit(solution)/shard_map/ppermute | solution.py:51
  31.8 41.0 %collective-permute-start.6 = (bf16[64,7680]{1,0:T(8,128)(2,1)S(1)}, bf16[64,7680]{1,0:T(8,128)(2,1)}, u32[]{:S(2)}, u32[]{:S(2)}) collective-permute-start(bf16[64,7680]{1,0:T(8,128)(2,1)S(1)} %join.2.refs_0_), channel_id=1, source_target_pairs={{0,1},{1,0},{2,3},{3,2},{4,5},{5,4},{6,7},{7,6},{8,9},{9,8},{10,11... | collective-permute-start | bytes 2949128 | tf_op jit(solution)/shard_map/ppermute | solution.py:51
  38.0 38.9 %all-to-all-start = ((bf16[16,16,512]{2,1,0:T(8,128)(2,1)}), bf16[16,16,512]{2,1,0:T(8,128)(2,1)S(1)}, u32[]{:S(2)}, u32[]{:S(2)}) async-start(bf16[16,16,512]{2,1,0:T(8,128)(2,1)} %bitcast.4), calls=%async_computation | async-start | bytes 524288 | tf_op jit(solution)/shard_map/all_to_all | solution.py:687
  58.3 13.4 %collective-permute-start.1 = (bf16[32,7680]{1,0:T(8,128)(2,1)}, bf16[32,7680]{1,0:T(8,128)(2,1)}, u32[]{:S(2)}, u32[]{:S(2)}) collective-permute-start(bf16[32,7680]{1,0:T(8,128)(2,1)} %copy-done), channel_id=1, source_target_pairs={{0,96},{32,64},{64,32},{96,0},{1,97},{33,65},{65,33},{97,1},{2,98}... | collective-permute-start | bytes 1474568 | tf_op jit(solution)/shard_map/ppermute | solution.py:39
  58.5 14.3 %collective-permute-start.3 = (bf16[32,7680]{1,0:T(8,128)(2,1)}, bf16[32,7680]{1,0:T(8,128)(2,1)}, u32[]{:S(2)}, u32[]{:S(2)}) collective-permute-start(bf16[32,7680]{1,0:T(8,128)(2,1)} %copy-done.1), channel_id=1, source_target_pairs={{0,32},{32,0},{64,96},{96,64},{1,33},{33,1},{65,97},{97,65},{2,34}... | collective-permute-start | bytes 1474568 | tf_op jit(solution)/shard_map/ppermute | solution.py:39
  71.6 8.5 %collective-permute-start.4 = (bf16[32,7680]{1,0:T(8,128)(2,1)}, bf16[32,7680]{1,0:T(8,128)(2,1)}, u32[]{:S(2)}, u32[]{:S(2)}) collective-permute-start(bf16[32,7680]{1,0:T(8,128)(2,1)} %collective-permute-done.1.refs_0_), channel_id=1, source_target_pairs={{0,1},{1,0},{2,3},{3,2},{4,5},{5,4},{6,7},{7,6},{8,9},{9,8},{10,11... | collective-permute-start | bytes 1474568 | tf_op jit(solution)/shard_map/ppermute | solution.py:51
  72.8 7.3 %collective-permute-start.5 = (bf16[32,7680]{1,0:T(8,128)(2,1)}, bf16[32,7680]{1,0:T(8,128)(2,1)}, u32[]{:S(2)}, u32[]{:S(2)}) collective-permute-start(bf16[32,7680]{1,0:T(8,128)(2,1)} %collective-permute-done.3.refs_1_), channel_id=1, source_target_pairs={{0,1},{1,0},{2,3},{3,2},{4,5},{5,4},{6,7},{7,6},{8,9},{9,8},{10,11... | collective-permute-start | bytes 1474568 | tf_op jit(solution)/shard_map/ppermute | solution.py:51
  72.8 88.7 %collective-permute-start.24 = (bf16[128,7168]{1,0:T(8,128)(2,1)}, bf16[128,7168]{1,0:T(8,128)(2,1)}, u32[]{:S(2)}, u32[]{:S(2)}) collective-permute-start(bf16[128,7168]{1,0:T(8,128)(2,1)} %down_a.1), channel_id=1, source_target_pairs={{0,1},{1,0},{2,3},{3,2},{4,5},{5,4},{6,7},{7,6},{8,9},{9,8},{10,11... | collective-permute-start | bytes 5505032 | tf_op jit(solution)/shard_map/ppermute | solution.py:51
  80.1 28.2 %copy-start.4 = (bf16[7168]{0:T(1024)(128)(2,1)S(1)}, bf16[7168]{0:T(1024)(128)(2,1)}, u32[]{:S(2)}) copy-start(bf16[7168]{0:T(1024)(128)(2,1)} %param.21) | copy-start | bytes 43012
  80.1 28.2 %copy-start.3 = (bf16[2,2,7168]{2,1,0:T(2,128)(2,1)S(1)}, bf16[2,2,7168]{2,1,0:T(2,128)(2,1)}, u32[]{:S(2)}) copy-start(bf16[2,2,7168]{2,1,0:T(2,128)(2,1)} %param.18) | copy-start | bytes 172036
  80.1 36.3 %copy-start.5 = (s32[2,2,8]{2,1,0:T(2,128)S(1)}, s32[2,2,8]{2,1,0:T(2,128)}, u32[]{:S(2)}) copy-start(s32[2,2,8]{2,1,0:T(2,128)} %param.23) | copy-start | bytes 388
  80.1 36.3 %copy-start.6 = (s32[2,2,8]{2,1,0:T(2,128)S(1)}, s32[2,2,8]{2,1,0:T(2,128)}, u32[]{:S(2)}) copy-start(s32[2,2,8]{2,1,0:T(2,128)} %param.24) | copy-start | bytes 388
  82.6 33.8 %copy-start.2 = (bf16[7168,16]{0,1:T(8,128)(2,1)S(1)}, bf16[7168,16]{0,1:T(8,128)(2,1)}, u32[]{:S(2)}) copy-start(bf16[7168,16]{0,1:T(8,128)(2,1)} %param.22) | copy-start | bytes 688132
  82.6 7.1 %collective-permute-start.12 = (bf16[32,1792]{1,0:T(8,128)(2,1)S(1)}, bf16[32,1792]{1,0:T(8,128)(2,1)S(1)}, u32[]{:S(2)}, u32[]{:S(2)}) collective-permute-start(bf16[32,1792]{1,0:T(8,128)(2,1)S(1)} %get-tuple-element.49), channel_id=1, source_target_pairs={{0,4},{2,6},{4,8},{6,10},{8,12},{10,14},{12,16},{14,18},{16,20},{1... | collective-permute-start | bytes 344072 | tf_op jit(solution)/shard_map/ppermute | solution.py:43
  84.2 12.5 %collective-permute-start.10 = (bf16[32,3584]{1,0:T(8,128)(2,1)S(1)}, bf16[32,3584]{1,0:T(8,128)(2,1)S(1)}, u32[]{:S(2)}, u32[]{:S(2)}) collective-permute-start(bf16[32,3584]{1,0:T(8,128)(2,1)S(1)} %get-tuple-element.47), channel_id=1, source_target_pairs={{0,2},{2,4},{4,6},{6,8},{8,10},{10,12},{12,14},{14,16},{16,18},{18... | collective-permute-start | bytes 688136 | tf_op jit(solution)/shard_map/ppermute | solution.py:43
  84.7 12.1 %collective-permute-start.11 = (bf16[32,3584]{1,0:T(8,128)(2,1)S(1)}, bf16[32,3584]{1,0:T(8,128)(2,1)S(1)}, u32[]{:S(2)}, u32[]{:S(2)}) collective-permute-start(bf16[32,3584]{1,0:T(8,128)(2,1)S(1)} %get-tuple-element.48), channel_id=1, source_target_pairs={{0,30},{2,0},{4,2},{6,4},{8,6},{10,8},{12,10},{14,12},{16,14},{18,... | collective-permute-start | bytes 688136 | tf_op jit(solution)/shard_map/ppermute | solution.py:43
  89.7 7.1 %collective-permute-start.13 = (bf16[32,1792]{1,0:T(8,128)(2,1)S(1)}, bf16[32,1792]{1,0:T(8,128)(2,1)S(1)}, u32[]{:S(2)}, u32[]{:S(2)}) collective-permute-start(bf16[32,1792]{1,0:T(8,128)(2,1)S(1)} %get-tuple-element.50), channel_id=1, source_target_pairs={{0,28},{2,30},{4,0},{6,2},{8,4},{10,6},{12,8},{14,10},{16,12},{18,... | collective-permute-start | bytes 344072 | tf_op jit(solution)/shard_map/ppermute | solution.py:43
  96.9 11.6 %collective-permute-start.14 = (bf16[8,3584]{1,0:T(8,128)(2,1)S(1)}, bf16[8,3584]{1,0:T(8,128)(2,1)S(1)}, u32[]{:S(2)}, u32[]{:S(2)}) collective-permute-start(bf16[8,3584]{1,0:T(8,128)(2,1)S(1)} %get-tuple-element.52), channel_id=1, source_target_pairs={{0,8},{8,0},{16,24},{24,16},{1,9},{9,1},{17,25},{25,17},{2,10},{10... | collective-permute-start | bytes 172040 | tf_op jit(solution)/shard_map/ppermute | solution.py:47
  102.3 14.1 %collective-permute-start.15 = (bf16[8,3584]{1,0:T(8,128)(2,1)S(1)}, bf16[8,3584]{1,0:T(8,128)(2,1)S(1)}, u32[]{:S(2)}, u32[]{:S(2)}) collective-permute-start(bf16[8,3584]{1,0:T(8,128)(2,1)S(1)} %get-tuple-element.53), channel_id=1, source_target_pairs={{0,16},{8,24},{16,0},{24,8},{1,17},{9,25},{17,1},{25,9},{2,18},{10... | collective-permute-start | bytes 172040 | tf_op jit(solution)/shard_map/ppermute | solution.py:47
  106.7 9.7 %collective-permute-start.16 = (bf16[8,3584]{1,0:T(8,128)(2,1)S(1)}, bf16[8,3584]{1,0:T(8,128)(2,1)S(1)}, u32[]{:S(2)}, u32[]{:S(2)}) collective-permute-start(bf16[8,3584]{1,0:T(8,128)(2,1)S(1)} %get-tuple-element.54), channel_id=1, source_target_pairs={{0,24},{8,16},{16,8},{24,0},{1,25},{9,17},{17,9},{25,1},{2,26},{10... | collective-permute-start | bytes 172040 | tf_op jit(solution)/shard_map/ppermute | solution.py:47
  139.6 6.2 %collective-permute-start.19 = (bf16[16,3712]{1,0:T(8,128)(2,1)S(1)}, bf16[16,3712]{1,0:T(8,128)(2,1)S(1)}, u32[]{:S(2)}, u32[]{:S(2)}) collective-permute-start(bf16[16,3712]{1,0:T(8,128)(2,1)S(1)} %get-tuple-element.83), channel_id=1, source_target_pairs={{0,4},{2,6},{4,8},{6,10},{8,12},{10,14},{12,16},{14,18},{16,20},{1... | collective-permute-start | bytes 356360 | tf_op jit(solution)/shard_map/ppermute | solution.py:43
  139.8 13.2 %collective-permute-start.20 = (bf16[32,3712]{1,0:T(8,128)(2,1)S(1)}, bf16[32,3712]{1,0:T(8,128)(2,1)S(1)}, u32[]{:S(2)}, u32[]{:S(2)}) collective-permute-start(bf16[32,3712]{1,0:T(8,128)(2,1)S(1)} %all_gather.3.refs_0_), channel_id=1, source_target_pairs={{0,2},{2,4},{4,6},{6,8},{8,10},{10,12},{12,14},{14,16},{16,18},{18... | collective-permute-start | bytes 712712 | tf_op jit(solution)/shard_map/ppermute | solution.py:43
  141.3 11.7 %collective-permute-start.17 = (bf16[32,3712]{1,0:T(8,128)(2,1)S(1)}, bf16[32,3712]{1,0:T(8,128)(2,1)S(1)}, u32[]{:S(2)}, u32[]{:S(2)}) collective-permute-start(bf16[32,3712]{1,0:T(8,128)(2,1)S(1)} %all_gather.3.refs_0_), channel_id=1, source_target_pairs={{0,30},{2,0},{4,2},{6,4},{8,6},{10,8},{12,10},{14,12},{16,14},{18,... | collective-permute-start | bytes 712712 | tf_op jit(solution)/shard_map/ppermute | solution.py:43
  145.9 7.1 %collective-permute-start.18 = (bf16[16,3712]{1,0:T(8,128)(2,1)S(1)}, bf16[16,3712]{1,0:T(8,128)(2,1)S(1)}, u32[]{:S(2)}, u32[]{:S(2)}) collective-permute-start(bf16[16,3712]{1,0:T(8,128)(2,1)S(1)} %get-tuple-element.84), channel_id=1, source_target_pairs={{0,28},{2,30},{4,0},{6,2},{8,4},{10,6},{12,8},{14,10},{16,12},{18,... | collective-permute-start | bytes 356360 | tf_op jit(solution)/shard_map/ppermute | solution.py:43
  154.2 19.9 %collective-permute-start.25 = (bf16[24,7296]{1,0:T(8,128)(2,1)S(1)}, bf16[24,7296]{1,0:T(8,128)(2,1)S(1)}, u32[]{:S(2)}, u32[]{:S(2)}) collective-permute-start(bf16[24,7296]{1,0:T(8,128)(2,1)S(1)} %get-tuple-element.64), channel_id=1, source_target_pairs={{0,32},{32,0},{64,96},{96,64},{1,33},{33,1},{65,97},{97,65},{2,34}... | collective-permute-start | bytes 1050632 | tf_op jit(solution)/shard_map/ppermute | solution.py:39
  159.0 15.0 %collective-permute-start.27 = (bf16[24,7296]{1,0:T(8,128)(2,1)S(1)}, bf16[24,7296]{1,0:T(8,128)(2,1)S(1)}, u32[]{:S(2)}, u32[]{:S(2)}) collective-permute-start(bf16[24,7296]{1,0:T(8,128)(2,1)S(1)} %get-tuple-element.66), channel_id=1, source_target_pairs={{0,96},{32,64},{64,32},{96,0},{1,97},{33,65},{65,33},{97,1},{2,98}... | collective-permute-start | bytes 1050632 | tf_op jit(solution)/shard_map/ppermute | solution.py:39
  160.6 9.0 %collective-permute-start.26 = (bf16[8,7296]{1,0:T(8,128)(2,1)S(1)}, bf16[8,7296]{1,0:T(8,128)(2,1)S(1)}, u32[]{:S(2)}, u32[]{:S(2)}) collective-permute-start(bf16[8,7296]{1,0:T(8,128)(2,1)S(1)} %get-tuple-element.65), channel_id=1, source_target_pairs={{0,32},{32,0},{64,96},{96,64},{1,33},{33,1},{65,97},{97,65},{2,34}... | collective-permute-start | bytes 350216 | tf_op jit(solution)/shard_map/ppermute | solution.py:39
  161.5 12.5 %collective-permute-start.28 = (bf16[8,7296]{1,0:T(8,128)(2,1)S(1)}, bf16[8,7296]{1,0:T(8,128)(2,1)S(1)}, u32[]{:S(2)}, u32[]{:S(2)}) collective-permute-start(bf16[8,7296]{1,0:T(8,128)(2,1)S(1)} %get-tuple-element.67), channel_id=1, source_target_pairs={{0,96},{32,64},{64,32},{96,0},{1,97},{33,65},{65,33},{97,1},{2,98}... | collective-permute-start | bytes 350216 | tf_op jit(solution)/shard_map/ppermute | solution.py:39
  162.8 17.9 %collective-permute-start.21 = (bf16[24,7296]{1,0:T(8,128)(2,1)S(1)}, bf16[24,7296]{1,0:T(8,128)(2,1)S(1)}, u32[]{:S(2)}, u32[]{:S(2)}) collective-permute-start(bf16[24,7296]{1,0:T(8,128)(2,1)S(1)} %get-tuple-element.59), channel_id=1, source_target_pairs={{0,64},{32,96},{64,0},{96,32},{1,65},{33,97},{65,1},{97,33},{2,66}... | collective-permute-start | bytes 1050632 | tf_op jit(solution)/shard_map/ppermute | solution.py:39
  169.7 11.1 %collective-permute-start.22 = (bf16[8,7296]{1,0:T(8,128)(2,1)S(1)}, bf16[8,7296]{1,0:T(8,128)(2,1)S(1)}, u32[]{:S(2)}, u32[]{:S(2)}) collective-permute-start(bf16[8,7296]{1,0:T(8,128)(2,1)S(1)} %get-tuple-element.60), channel_id=1, source_target_pairs={{0,64},{32,96},{64,0},{96,32},{1,65},{33,97},{65,1},{97,33},{2,66}... | collective-permute-start | bytes 350216 | tf_op jit(solution)/shard_map/ppermute | solution.py:39
  176.9 11.9 %collective-permute-start.32 = (bf16[24,7168]{1,0:T(8,128)(2,1)S(1)}, bf16[24,7168]{1,0:T(8,128)(2,1)S(1)}, u32[]{:S(2)}, u32[]{:S(2)}) collective-permute-start(bf16[24,7168]{1,0:T(8,128)(2,1)S(1)} %get-tuple-element.72), channel_id=1, source_target_pairs={{0,32},{32,0},{64,96},{96,64},{1,33},{33,1},{65,97},{97,65},{2,34}... | collective-permute-start | bytes 1032200 | tf_op jit(solution)/shard_map/ppermute | solution.py:39
  177.0 16.8 %collective-permute-start.33 = (bf16[24,7168]{1,0:T(8,128)(2,1)S(1)}, bf16[24,7168]{1,0:T(8,128)(2,1)S(1)}, u32[]{:S(2)}, u32[]{:S(2)}) collective-permute-start(bf16[24,7168]{1,0:T(8,128)(2,1)S(1)} %get-tuple-element.73), channel_id=1, source_target_pairs={{0,96},{32,64},{64,32},{96,0},{1,97},{33,65},{65,33},{97,1},{2,98}... | collective-permute-start | bytes 1032200 | tf_op jit(solution)/shard_map/ppermute | solution.py:39
  183.6 10.3 %collective-permute-start.34 = (bf16[24,7168]{1,0:T(8,128)(2,1)S(1)}, bf16[24,7168]{1,0:T(8,128)(2,1)S(1)}, u32[]{:S(2)}, u32[]{:S(2)}) collective-permute-start(bf16[24,7168]{1,0:T(8,128)(2,1)S(1)} %get-tuple-element.74), channel_id=1, source_target_pairs={{0,64},{32,96},{64,0},{96,32},{1,65},{33,97},{65,1},{97,33},{2,66}... | collective-permute-start | bytes 1032200 | tf_op jit(solution)/shard_map/ppermute | solution.py:39
  186.4 13.2 %collective-permute-start.29 = (bf16[8,7168]{1,0:T(8,128)(2,1)S(1)}, bf16[8,7168]{1,0:T(8,128)(2,1)S(1)}, u32[]{:S(2)}, u32[]{:S(2)}) collective-permute-start(bf16[8,7168]{1,0:T(8,128)(2,1)S(1)} %get-tuple-element.68), channel_id=1, source_target_pairs={{0,32},{32,0},{64,96},{96,64},{1,33},{33,1},{65,97},{97,65},{2,34}... | collective-permute-start | bytes 344072 | tf_op jit(solution)/shard_map/ppermute | solution.py:39
  187.1 19.0 %collective-permute-start.30 = (bf16[8,7168]{1,0:T(8,128)(2,1)S(1)}, bf16[8,7168]{1,0:T(8,128)(2,1)S(1)}, u32[]{:S(2)}, u32[]{:S(2)}) collective-permute-start(bf16[8,7168]{1,0:T(8,128)(2,1)S(1)} %get-tuple-element.69), channel_id=1, source_target_pairs={{0,96},{32,64},{64,32},{96,0},{1,97},{33,65},{65,33},{97,1},{2,98}... | collective-permute-start | bytes 344072 | tf_op jit(solution)/shard_map/ppermute | solution.py:39
  194.2 21.0 %collective-permute-start.35 = (bf16[32,3584]{1,0:T(8,128)(2,1)S(1)}, bf16[32,3584]{1,0:T(8,128)(2,1)S(1)}, u32[]{:S(2)}, u32[]{:S(2)}) collective-permute-start(bf16[32,3584]{1,0:T(8,128)(2,1)S(1)} %get-tuple-element.75), channel_id=1, source_target_pairs={{0,2},{2,4},{4,6},{6,8},{8,10},{10,12},{12,14},{14,16},{16,18},{18... | collective-permute-start | bytes 688136 | tf_op jit(solution)/shard_map/ppermute | solution.py:43
  196.1 19.1 %collective-permute-start.36 = (bf16[32,3584]{1,0:T(8,128)(2,1)S(1)}, bf16[32,3584]{1,0:T(8,128)(2,1)S(1)}, u32[]{:S(2)}, u32[]{:S(2)}) collective-permute-start(bf16[32,3584]{1,0:T(8,128)(2,1)S(1)} %get-tuple-element.76), channel_id=1, source_target_pairs={{0,30},{2,0},{4,2},{6,4},{8,6},{10,8},{12,10},{14,12},{16,14},{18,... | collective-permute-start | bytes 688136 | tf_op jit(solution)/shard_map/ppermute | solution.py:43
  196.4 11.5 %collective-permute-start.31 = (bf16[8,7168]{1,0:T(8,128)(2,1)S(1)}, bf16[8,7168]{1,0:T(8,128)(2,1)S(1)}, u32[]{:S(2)}, u32[]{:S(2)}) collective-permute-start(bf16[8,7168]{1,0:T(8,128)(2,1)S(1)} %get-tuple-element.70), channel_id=1, source_target_pairs={{0,64},{32,96},{64,0},{96,32},{1,65},{33,97},{65,1},{97,33},{2,66}... | collective-permute-start | bytes 344072 | tf_op jit(solution)/shard_map/ppermute | solution.py:39
  199.6 11.4 %collective-permute-start.37 = (bf16[32,1792]{1,0:T(8,128)(2,1)S(1)}, bf16[32,1792]{1,0:T(8,128)(2,1)S(1)}, u32[]{:S(2)}, u32[]{:S(2)}) collective-permute-start(bf16[32,1792]{1,0:T(8,128)(2,1)S(1)} %get-tuple-element.77), channel_id=1, source_target_pairs={{0,4},{2,6},{4,8},{6,10},{8,12},{10,14},{12,16},{14,18},{16,20},{1... | collective-permute-start | bytes 344072 | tf_op jit(solution)/shard_map/ppermute | solution.py:43
  206.1 9.1 %collective-permute-start.38 = (bf16[32,1792]{1,0:T(8,128)(2,1)S(1)}, bf16[32,1792]{1,0:T(8,128)(2,1)S(1)}, u32[]{:S(2)}, u32[]{:S(2)}) collective-permute-start(bf16[32,1792]{1,0:T(8,128)(2,1)S(1)} %get-tuple-element.78), channel_id=1, source_target_pairs={{0,28},{2,30},{4,0},{6,2},{8,4},{10,6},{12,8},{14,10},{16,12},{18,... | collective-permute-start | bytes 344072 | tf_op jit(solution)/shard_map/ppermute | solution.py:43
  215.4 13.3 %collective-permute-start.39 = (bf16[8,3584]{1,0:T(8,128)(2,1)S(1)}, bf16[8,3584]{1,0:T(8,128)(2,1)S(1)}, u32[]{:S(2)}, u32[]{:S(2)}) collective-permute-start(bf16[8,3584]{1,0:T(8,128)(2,1)S(1)} %get-tuple-element.80), channel_id=1, source_target_pairs={{0,8},{8,0},{16,24},{24,16},{1,9},{9,1},{17,25},{25,17},{2,10},{10... | collective-permute-start | bytes 172040 | tf_op jit(solution)/shard_map/ppermute | solution.py:47
  218.4 13.0 %collective-permute-start.40 = (bf16[8,3584]{1,0:T(8,128)(2,1)S(1)}, bf16[8,3584]{1,0:T(8,128)(2,1)S(1)}, u32[]{:S(2)}, u32[]{:S(2)}) collective-permute-start(bf16[8,3584]{1,0:T(8,128)(2,1)S(1)} %get-tuple-element.81), channel_id=1, source_target_pairs={{0,16},{8,24},{16,0},{24,8},{1,17},{9,25},{17,1},{25,9},{2,18},{10... | collective-permute-start | bytes 172040 | tf_op jit(solution)/shard_map/ppermute | solution.py:47
  228.7 8.1 %collective-permute-start.41 = (bf16[8,3584]{1,0:T(8,128)(2,1)S(1)}, bf16[8,3584]{1,0:T(8,128)(2,1)S(1)}, u32[]{:S(2)}, u32[]{:S(2)}) collective-permute-start(bf16[8,3584]{1,0:T(8,128)(2,1)S(1)} %get-tuple-element.82), channel_id=1, source_target_pairs={{0,24},{8,16},{16,8},{24,0},{1,25},{9,17},{17,9},{25,1},{2,26},{10... | collective-permute-start | bytes 172040 | tf_op jit(solution)/shard_map/ppermute | solution.py:47
where the time goes:
time: 238 us; the launch traced here: 237 us
  starting transfers between devices  92.4 us (39%)
  waiting for transfers between devices  88.7 us (37%)
  Pallas kernels  32.5 us (14%)
  blocking collectives  22.6 us (9%)
    ppermute x18, waiting for transfers between devices, swap_x(): lax.ppermute(a, 'x', [(i, i ^ bits) for i in range(lax.axis_size('x'))])  43.2 us
    ppermute x18, starting transfers between devices, swap_x(): lax.ppermute(a, 'x', [(i, i ^ bits) for i in range(lax.axis_size('x'))])  27.7 us
    ppermute x12, waiting for transfers between devices, shift_z(): return lax.ppermute(a, ZAX, [(i, (i + step) % RING) for i in range(RING)])  26.1 us
    ppermute x6, starting transfers between devices, swap_far(): return lax.ppermute(a, 'zb', [(i, i ^ bits) for i in range(FAR)])  24.7 us
    all_gather x1, blocking collectives, layer(): ring = lax.all_gather(payload, 'zb', axis=0, tiled=True)  22.6 us
    all_to_all x1, starting transfers between devices, layer(): lax.all_to_all(outgoing.reshape(RING, nx * tok, LAT), ZAX, split_axis=0,...  20.3 us
    ppermute x12, starting transfers between devices, shift_z(): return lax.ppermute(a, ZAX, [(i, (i + step) % RING) for i in range(RING)])  18.4 us
    ppermute x6, waiting for transfers between devices, swap_far(): return lax.ppermute(a, 'zb', [(i, i ^ bits) for i in range(FAR)])  16 us
  transfers between devices with their start and end apart: 43, of which 19 were waited for; matrix products, arithmetic and copies ran while one was open for 0% of the time, Pallas kernels for 13%

commit v1 on v0

--- a/solution.py
+++ b/solution.py
@@ -305,6 +305,29 @@
     )(where, arrived, *pieces, *([before] if last else []))
 
 
+def ring_kernel(where_ref, *refs):
+    parts, (whole, lower, upper) = refs[:FAR], refs[FAR:]
+    rows, middle = parts[0].shape[0], lower.shape[0]
+    for bits, part in enumerate(parts):
+        whole[pl.ds(pl.multiple_of((where_ref[1] ^ bits) * rows, rows), rows)] = part[...]
+    lower[...] = whole[pl.ds(0, middle)]
+    upper[...] = whole[pl.ds(middle, middle)]
+
+
+def ring_of(where, parts):
+    rows, width = parts[0].shape
+    shapes = [(FAR * rows, width), (FAR * rows // 2, width), (FAR * rows // 2, width)]
+    return pl.pallas_call(
+        ring_kernel,
+        out_shape=[jax.ShapeDtypeStruct(shape, bf16) for shape in shapes],
+        in_specs=[smem()] + [vmem()] * FAR,
+        out_specs=[vmem()] * 3,
+        compiler_params=params(4),
+        cost_estimate=cost(rows * width, 12 * rows * width),
+        name="ring",
+    )(where, *parts)
+
+
 SEND_TILE = 512
 
 
@@ -395,7 +418,7 @@
     )(where, *tokens)
 
 
-CHUNKS = 14
+CHUNKS = 7
 
 
 def pair_kernel(first, second, out, sem):
@@ -459,17 +482,16 @@
 
 
 def expert_kernel(groups, where_ref, *refs):
-    tokens, refs = refs[: 2 * groups], refs[2 * groups :]
-    (wide, deep), (early, late) = refs[:2], (refs[2 : groups + 2], refs[groups + 2 : -1])
-    held = refs[-1]
+    tokens = refs[:groups]
+    wide, deep = refs[groups : groups + 2]
+    early, late = refs[groups + 2 : 2 * groups + 2], refs[2 * groups + 2 : 3 * groups + 2]
+    held = refs[3 * groups + 2] if groups > 1 else tokens[0]
     dim = wide.shape[0]
     part = wide.shape[1] // 2
     chunk = dim // CHUNKS
-    chunks = CHUNKS
-    for g in range(groups):
-        held[pl.ds(g * SLOTS, EARLY)] = tokens[2 * g][...]
-        held[pl.ds(g * SLOTS + EARLY, LATE)] = tokens[2 * g + 1][...]
-
+    if groups > 1:
+        for g, ref in enumerate(tokens):
+            held[pl.ds(g * SLOTS, SLOTS)] = ref[...]
     total = jnp.dot(held[:, pl.ds(0, dim)], wide[...], preferred_element_type=f32)
     gate, upward = total[:, :part], total[:, part:]
     act = (gate / (1.0 + jnp.exp(-gate)) * upward).astype(bf16)
@@ -478,30 +500,28 @@
     from_share = iota(shape, 0) - CAP * EXPERTS
     hot = (from_share >= 0) & (from_share < 3 * EXPERTS) & (lax.rem(from_share + EXTRA, EXPERTS) == expert)
     share = jnp.dot(held[:, pl.ds(dim, EXTRA)], one_hot(hot), preferred_element_type=f32)[:, :1]
-
-    @pl.loop(0, 2)
-    def _(i):
-        for k in range(chunks // 2):
-            cols = pl.ds(pl.multiple_of((i * (chunks // 2) + k) * chunk, chunk), chunk)
-            got = jnp.dot(act, deep[:, cols], preferred_element_type=f32) * share
-            for g in range(groups):
-                rows = got[g * SLOTS : (g + 1) * SLOTS].astype(bf16)
-                early[g][:, cols] = rows[:EARLY]
-                late[g][:, cols] = rows[EARLY:]
+    for k in range(CHUNKS):
+        cols = pl.ds(k * chunk, chunk)
+        got = jnp.dot(act, deep[:, cols], preferred_element_type=f32) * share
+        for g in range(groups):
+            rows = got[g * SLOTS : (g + 1) * SLOTS].astype(bf16)
+            early[g][:, cols] = rows[:EARLY]
+            late[g][:, cols] = rows[EARLY:]
 
 
 def expert_part(where, tokens, weights):
     wide, deep = weights
     dim = wide.shape[0]
-    groups = len(tokens) // 2
+    groups = len(tokens)
     rows = groups * SLOTS
+    held = [pltpu.VMEM((rows, dim + EXTRA), bf16)] if groups > 1 else []
     return pl.pallas_call(
         functools.partial(expert_kernel, groups),
         out_shape=(jax.ShapeDtypeStruct((EARLY, dim), bf16),) * groups
         + (jax.ShapeDtypeStruct((LATE, dim), bf16),) * groups,
-        in_specs=[smem()] + [vmem()] * (2 * groups + 2),
+        in_specs=[smem()] + [vmem()] * (groups + 2),
         out_specs=[vmem()] * (2 * groups),
-        scratch_shapes=[pltpu.VMEM((rows, dim + EXTRA), bf16)],
+        scratch_shapes=held,
         compiler_params=params(8),
         cost_estimate=cost(6 * rows * wide.size, 2 * rows * dim),
         name="expert_part",
@@ -710,23 +730,16 @@
     ]
     hidden, payload = route(added, rows, gain, router.T, ids, places)
 
-    ring = lax.all_gather(payload, "zb", axis=0, tiled=True)
-    middle = ring.shape[0] // 2
-    above, below = shift_z(ring, -1), shift_z(ring, 1)
-    beyond = shift_z(ring[:middle], -2), shift_z(ring[middle:], 2)
-    near = (above, *beyond, below)
-    sent = dispatch(where, nx, (ring,), tok)
-    late_in = [swap_x(sent[i], COLUMNS[i]) for i in range(1, nx)]
-    late_in = [sent[0], *late_in]
-    sent = dispatch(where, nx, near, tok)
-    early_in = [swap_x(sent[i], COLUMNS[i]) for i in range(1, nx)]
-    early_in = [sent[0], *early_in]
+    ring, lower, upper = ring_of(where, [payload] + [swap_far(payload, k) for k in range(1, FAR)])
+    near = shift_z(ring, -1), shift_z(lower, -2), shift_z(upper, 2), shift_z(ring, 1)
+    sent = dispatch(where, nx, (*near, ring), tok)
+    got = [swap_x(sent[i], COLUMNS[i]) for i in range(1, nx)]
     late = plan(where, nx, (ring,), tok, 0, 1, 0)
     early = plan(where, nx, near, tok, 1, len(STEPS) - 1, 1)
-    got = [pair for pairs in zip(early_in, late_in) for pair in pairs]
-    first = expert_part(where, got[2:6], weights)
-    second = expert_part(where, got[:2] + got[6:], weights)
-    done = [[second[2 * n], *first[2 * n : 2 * n + 2], second[2 * n + 1]] for n in range(2)]
+    done = expert_part(where, (sent[0], *got[: nx - 2]), weights)
+    done = [list(done[: nx - 1]), list(done[nx - 1 :])]
+    for rows, last in zip(done, expert_part(where, got[nx - 2 :], weights)):
+        rows.append(last)
     first = [done[0][0]] + [swap_x(done[0][i], COLUMNS[i]) for i in range(1, nx)]
     second = [done[1][0]] + [swap_x(done[1][i], COLUMNS[i]) for i in range(1, nx)]
     added = reduce_z((late, *second), *collect(early, first))

time: 238 us -> 239 us (level)
  the two profiles are of different devices: /device:TPU:426 before, /device:TPU:164 now
where the time goes in v1:
time: 239 us; the launch traced here: 238 us
  starting transfers between devices  104 us (44%)
  waiting for transfers between devices  100 us (42%)
  Pallas kernels  32.9 us (14%)
    ppermute x15, waiting for transfers between devices, swap_x(): lax.ppermute(a, 'x', [(i, i ^ bits) for i in range(lax.axis_size('x'))])  47.5 us
    ppermute x9, starting transfers between devices, swap_far(): return lax.ppermute(a, 'zb', [(i, i ^ bits) for i in range(FAR)])  35.6 us
    ppermute x12, waiting for transfers between devices, shift_z(): return lax.ppermute(a, ZAX, [(i, (i + step) % RING) for i in range(RING)])  25.3 us
    ppermute x9, waiting for transfers between devices, swap_far(): return lax.ppermute(a, 'zb', [(i, i ^ bits) for i in range(FAR)])  23.8 us
    ppermute x15, starting transfers between devices, swap_x(): lax.ppermute(a, 'x', [(i, i ^ bits) for i in range(lax.axis_size('x'))])  23.5 us
    all_to_all x1, starting transfers between devices, layer(): lax.all_to_all(outgoing.reshape(RING, nx * tok, LAT), ZAX, split_axis=0,...  22.9 us
    ppermute x12, starting transfers between devices, shift_z(): return lax.ppermute(a, ZAX, [(i, (i + step) % RING) for i in range(RING)])  20.7 us
    pallas_call x1, Pallas kernels, context_rows(): pl.pallas_call(functools.partial(context_kernel, nx), grid=(seqs,), out_s...  5.88 us
  transfers between devices with their start and end apart: 43, of which 19 were waited for; matrix products, arithmetic and copies ran while one was open for 0% of the time, Pallas kernels for 12%

profile of v1, /device:TPU:164, one launch (start us, length us, event | category | flops | bytes accessed | tf_op | source)
XLA Modules:
  0.0 237.5 jit_solution(3030152859452183074)
XLA Ops:
  0.0 3.9 %pair.1 = bf16[14336,128]{1,0:T(8,128)(2,1)} custom-call(bf16[7168,128]{1,0:T(8,128)(2,1)} %gate.1, bf16[7168,128]{1,0:T(8,128)(2,1)} %up.1), custom_call_target="tpu_custom_call" | custom-call | flops 1 | bytes 7340032 | tf_op jit(solution)/shard_map/pair/pallas_call | solution.py:438
  4.0 1.2 pack.1
  5.2 0.5 collective-permute-start.8
  5.8 1.1 collective-permute-start
  6.8 0.9 collective-permute-start.7
  7.8 1.6 collective-permute-start.2
  9.4 10.0 %collective-permute-done.8.refs_2_ = bf16[32,7680]{1,0:T(8,128)(2,1)S(1)} collective-permute-done((bf16[32,7680]{1,0:T(8,128)(2,1)S(1)}, bf16[32,7680]{1,0:T(8,128)(2,1)S(1)}, u32[]{:S(2)}, u32[]{:S(2)}) %collective-permute-start.8) | collective-permute-done | bytes 491552 | tf_op jit(solution)/shard_map/ppermute | solution.py:39
  19.5 0.5 collective-permute-done.refs_0_
  20.0 9.7 %collective-permute-done.7.refs_1_ = bf16[32,7680]{1,0:T(8,128)(2,1)S(1)} collective-permute-done((bf16[32,7680]{1,0:T(8,128)(2,1)S(1)}, bf16[32,7680]{1,0:T(8,128)(2,1)S(1)}, u32[]{:S(2)}, u32[]{:S(2)}) %collective-permute-start.7) | collective-permute-done | bytes 491552 | tf_op jit(solution)/shard_map/ppermute | solution.py:39
  29.7 1.3 join.3.refs_2_
  31.2 1.9 collective-permute-start.1
  33.4 5.9 %context_rows.1 = bf16[256,512]{1,0:T(8,128)(2,1)} custom-call(s32[5]{0:T(128)S(1)} %pad_add_fusion.where_ref, bf16[2,576,2048]{2,1,0:T(8,128)(2,1)} %bitcast.20, bf16[2,2,64,576]{3,2,1,0:T(8,128)(2,1)} %queries.1, bf16[2,2,576]{2,1,0:T(2,128)(2,1)} %new.1), custom_call_target="tpu_custom_call" | custom-call | flops 1140850688 | bytes 4718592 | tf_op jit(solution)/shard_map/context_rows/pallas_call | solution.py:165
  39.3 22.9 %all-to-all-start = ((bf16[16,16,512]{2,1,0:T(8,128)(2,1)}), bf16[16,16,512]{2,1,0:T(8,128)(2,1)S(1)}, u32[]{:S(2)}, u32[]{:S(2)}) async-start(bf16[16,16,512]{2,1,0:T(8,128)(2,1)} %bitcast.4), calls=%async_computation | async-start | bytes 524288 | tf_op jit(solution)/shard_map/all_to_all | solution.py:707
  62.3 2.5 %collective-permute-start.3 = (bf16[32,7680]{1,0:T(8,128)(2,1)}, bf16[32,7680]{1,0:T(8,128)(2,1)}, u32[]{:S(2)}, u32[]{:S(2)}) collective-permute-start(bf16[32,7680]{1,0:T(8,128)(2,1)} %copy-done), channel_id=1, source_target_pairs={{0,32},{32,0},{64,96},{96,64},{1,33},{33,1},{65,97},{97,65},{2,34}... | collective-permute-start | bytes 1474568 | tf_op jit(solution)/shard_map/ppermute | solution.py:39
  64.8 12.1 %collective-permute-done.3.refs_1_ = bf16[32,7680]{1,0:T(8,128)(2,1)} collective-permute-done((bf16[32,7680]{1,0:T(8,128)(2,1)}, bf16[32,7680]{1,0:T(8,128)(2,1)}, u32[]{:S(2)}, u32[]{:S(2)}) %collective-permute-start.3) | collective-permute-done | bytes 491552 | tf_op jit(solution)/shard_map/ppermute | solution.py:39
  76.8 0.5 collective-permute-start.5
  77.3 3.6 %all-to-all-done = bf16[16,16,512]{2,1,0:T(8,128)(2,1)S(1)} async-done(((bf16[16,16,512]{2,1,0:T(8,128)(2,1)}), bf16[16,16,512]{2,1,0:T(8,128)(2,1)S(1)}, u32[]{:S(2)}, u32[]{:S(2)}) %all-to-all-start) | async-done | bytes 262176 | tf_op jit(solution)/shard_map/all_to_all | solution.py:707
  80.9 3.2 %attend_part.2.refs_4_ = f32[128,3584]{1,0:T(8,128)S(1)} custom-call(s32[5]{0:T(128)S(1)} %pad_add_fusion.where_ref, bf16[256,512]{1,0:T(8,128)(2,1)S(1)} %bitcast.15, bf16[64,7680]{1,0:T(8,128)(2,1)S(1)} %join.2.refs_0_, bf16[64,7680]{1,0:T(8,128)(2,1)} %collective-permute-done.6.refs_1_, bf16[128,7680]{1,0:T(8,128)(2,1)S(1)} %join.3.refs_2_, ...), custom_call_target="tpu_custom_call" | custom-call | flops 1409286144 | bytes 5505024 | tf_op jit(solution)/shard_map/attend_part/pallas_call | solution.py:297
  84.2 2.4 %attend_part.3 = (f32[32,3584]{1,0:T(8,128)S(1)}, bf16[32,3584]{1,0:T(8,128)(2,1)S(1)}, bf16[32,3584]{1,0:T(8,128)(2,1)S(1)}, bf16[32,1792]{1,0:T(8,128)(2,1)S(1)}, bf16[32,1792]{1,0:T(8,128)(2,1)S(1)}) custom-call(s32[5]{0:T(128)S(1)} %pad_add_fusion.where_ref, bf16[256,512]{1,0:T(8,128)(2,1)S(1)} %bitcast.16, ...), custom_call_target="tpu_custom_call" | custom-call | flops 469762048 | bytes 1835008 | tf_op jit(solution)/shard_map/attend_part/pallas_call | solution.py:297
  86.6 2.3 collective-permute-start.12
  89.2 1.8 collective-permute-start.11
  91.0 4.9 %collective-permute-done.12.refs_3_ = bf16[32,1792]{1,0:T(8,128)(2,1)S(1)} collective-permute-done((bf16[32,1792]{1,0:T(8,128)(2,1)S(1)}, bf16[32,1792]{1,0:T(8,128)(2,1)S(1)}, u32[]{:S(2)}, u32[]{:S(2)}) %collective-permute-start.12) | collective-permute-done | bytes 114720 | tf_op jit(solution)/shard_map/ppermute | solution.py:43
  96.0 2.1 collective-permute-start.13
  98.0 4.2 %collective-permute-done.13.refs_4_ = bf16[32,1792]{1,0:T(8,128)(2,1)S(1)} collective-permute-done((bf16[32,1792]{1,0:T(8,128)(2,1)S(1)}, bf16[32,1792]{1,0:T(8,128)(2,1)S(1)}, u32[]{:S(2)}, u32[]{:S(2)}) %collective-permute-start.13) | collective-permute-done | bytes 114720 | tf_op jit(solution)/shard_map/ppermute | solution.py:43
  102.4 2.2 collective-permute-start.14
  104.6 6.7 %collective-permute-start.15 = (bf16[8,3584]{1,0:T(8,128)(2,1)S(1)}, bf16[8,3584]{1,0:T(8,128)(2,1)S(1)}, u32[]{:S(2)}, u32[]{:S(2)}) collective-permute-start(bf16[8,3584]{1,0:T(8,128)(2,1)S(1)} %get-tuple-element.52), channel_id=1, source_target_pairs={{0,16},{8,24},{16,0},{24,8},{1,17},{9,25},{17,1},{25,9},{2,18},{10... | collective-permute-start | bytes 172040 | tf_op jit(solution)/shard_map/ppermute | solution.py:47
  111.4 2.5 %collective-permute-start.16 = (bf16[8,3584]{1,0:T(8,128)(2,1)S(1)}, bf16[8,3584]{1,0:T(8,128)(2,1)S(1)}, u32[]{:S(2)}, u32[]{:S(2)}) collective-permute-start(bf16[8,3584]{1,0:T(8,128)(2,1)S(1)} %get-tuple-element.53), channel_id=1, source_target_pairs={{0,24},{8,16},{16,8},{24,0},{1,25},{9,17},{17,9},{25,1},{2,26},{10... | collective-permute-start | bytes 172040 | tf_op jit(solution)/shard_map/ppermute | solution.py:47
  114.0 4.8 %collective-permute-done.15.two = bf16[8,3584]{1,0:T(8,128)(2,1)S(1)} collective-permute-done((bf16[8,3584]{1,0:T(8,128)(2,1)S(1)}, bf16[8,3584]{1,0:T(8,128)(2,1)S(1)}, u32[]{:S(2)}, u32[]{:S(2)}) %collective-permute-start.15) | collective-permute-done | bytes 57376 | tf_op jit(solution)/shard_map/ppermute | solution.py:47
  118.9 0.9 collective-permute-done.16.three
  119.8 0.6 route.1
  120.5 4.6 %collective-permute-start.19 = (bf16[8,3712]{1,0:T(8,128)(2,1)S(1)}, bf16[8,3712]{1,0:T(8,128)(2,1)S(1)}, u32[]{:S(2)}, u32[]{:S(2)}) collective-permute-start(bf16[8,3712]{1,0:T(8,128)(2,1)S(1)} %get-tuple-element.55.refs_0_), channel_id=1, source_target_pairs={{0,24},{8,16},{16,8},{24,0},{1,25},{9,17},{17,9},{25,1},{2,26},{10... | collective-permute-start | bytes 178184 | tf_op jit(solution)/shard_map/ppermute | solution.py:47
  125.0 6.3 %collective-permute-start.18 = (bf16[8,3712]{1,0:T(8,128)(2,1)S(1)}, bf16[8,3712]{1,0:T(8,128)(2,1)S(1)}, u32[]{:S(2)}, u32[]{:S(2)}) collective-permute-start(bf16[8,3712]{1,0:T(8,128)(2,1)S(1)} %get-tuple-element.55.refs_0_), channel_id=1, source_target_pairs={{0,16},{8,24},{16,0},{24,8},{1,17},{9,25},{17,1},{25,9},{2,18},{10... | collective-permute-start | bytes 178184 | tf_op jit(solution)/shard_map/ppermute | solution.py:47
  131.4 0.4 collective-permute-start.17
  131.8 6.6 %collective-permute-done.18.refs_2_ = bf16[8,3712]{1,0:T(8,128)(2,1)S(1)} collective-permute-done((bf16[8,3712]{1,0:T(8,128)(2,1)S(1)}, bf16[8,3712]{1,0:T(8,128)(2,1)S(1)}, u32[]{:S(2)}, u32[]{:S(2)}) %collective-permute-start.18) | collective-permute-done | bytes 59424 | tf_op jit(solution)/shard_map/ppermute | solution.py:47
  138.4 3.2 %collective-permute-done.17.refs_1_ = bf16[8,3712]{1,0:T(8,128)(2,1)S(1)} collective-permute-done((bf16[8,3712]{1,0:T(8,128)(2,1)S(1)}, bf16[8,3712]{1,0:T(8,128)(2,1)S(1)}, u32[]{:S(2)}, u32[]{:S(2)}) %collective-permute-start.17) | collective-permute-done | bytes 59424 | tf_op jit(solution)/shard_map/ppermute | solution.py:47
  141.6 0.6 ring.1
  142.2 3.6 %collective-permute-start.21 = (bf16[16,3712]{1,0:T(8,128)(2,1)S(1)}, bf16[16,3712]{1,0:T(8,128)(2,1)S(1)}, u32[]{:S(2)}, u32[]{:S(2)}) collective-permute-start(bf16[16,3712]{1,0:T(8,128)(2,1)S(1)} %get-tuple-element.57), channel_id=1, source_target_pairs={{0,28},{2,30},{4,0},{6,2},{8,4},{10,6},{12,8},{14,10},{16,12},{18,... | collective-permute-start | bytes 356360 | tf_op jit(solution)/shard_map/ppermute | solution.py:43
  145.9 2.0 collective-permute-start.20
  147.8 4.0 %collective-permute-done.21.refs_1_ = bf16[16,3712]{1,0:T(8,128)(2,1)S(1)} collective-permute-done((bf16[16,3712]{1,0:T(8,128)(2,1)S(1)}, bf16[16,3712]{1,0:T(8,128)(2,1)S(1)}, u32[]{:S(2)}, u32[]{:S(2)}) %collective-permute-start.21) | collective-permute-done | bytes 118816 | tf_op jit(solution)/shard_map/ppermute | solution.py:43
  151.8 6.9 %collective-permute-done.22.refs_2_ = bf16[16,3712]{1,0:T(8,128)(2,1)S(1)} collective-permute-done((bf16[16,3712]{1,0:T(8,128)(2,1)S(1)}, bf16[16,3712]{1,0:T(8,128)(2,1)S(1)}, u32[]{:S(2)}, u32[]{:S(2)}) %collective-permute-start.22) | collective-permute-done | bytes 118816 | tf_op jit(solution)/shard_map/ppermute | solution.py:43
  158.8 1.3 dispatch.1
  160.1 3.3 %collective-permute-start.24 = (bf16[32,7296]{1,0:T(8,128)(2,1)S(1)}, bf16[32,7296]{1,0:T(8,128)(2,1)S(1)}, u32[]{:S(2)}, u32[]{:S(2)}) collective-permute-start(bf16[32,7296]{1,0:T(8,128)(2,1)S(1)} %get-tuple-element.60), channel_id=1, source_target_pairs={{0,32},{32,0},{64,96},{96,64},{1,33},{33,1},{65,97},{97,65},{2,34}... | collective-permute-start | bytes 1400840 | tf_op jit(solution)/shard_map/ppermute | solution.py:39
  163.4 2.2 collective-permute-start.30
  165.6 4.2 %stage.1 = (bf16[7168,512]{1,0:T(8,128)(2,1)S(1)}, bf16[256,7168]{1,0:T(8,128)(2,1)S(1)}) custom-call(bf16[7168,128]{1,0:T(8,128)(2,1)} %gate.1, bf16[7168,128]{1,0:T(8,128)(2,1)} %up.1, bf16[14336,128]{1,0:T(8,128)(2,1)} %collective-permute-done.26.others, bf16[128,7168]{1,0:T(8,128)(2,1)} %down_a.1, bf16[128,7168]{1,0:T(8,128)(2,1)} %collective-permute-done.27.down_b), custom_call_target="tpu_custom_call" | custom-call | flops 3670016000 | bytes 11010048 | tf_op jit(solution)/shard_map/stage/pallas_call | solution.py:469
  169.9 1.4 collective-permute-done.24.refs_1_
  171.3 10.1 %collective-permute-done.25.refs_2_ = bf16[32,7296]{1,0:T(8,128)(2,1)S(1)} collective-permute-done((bf16[32,7296]{1,0:T(8,128)(2,1)S(1)}, bf16[32,7296]{1,0:T(8,128)(2,1)S(1)}, u32[]{:S(2)}, u32[]{:S(2)}) %collective-permute-start.25) | collective-permute-done | bytes 466976 | tf_op jit(solution)/shard_map/ppermute | solution.py:39
  181.4 2.5 %expert_part.2 = (bf16[24,7168]{1,0:T(8,128)(2,1)S(1)}, bf16[24,7168]{1,0:T(8,128)(2,1)S(1)}, bf16[24,7168]{1,0:T(8,128)(2,1)S(1)}, bf16[8,7168]{1,0:T(8,128)(2,...) custom-call(s32[5]{0:T(128)S(1)} %pad_add_fusion.where_ref, ...), custom_call_target="tpu_custom_call" | custom-call | flops 2113929216 | bytes 1376256 | tf_op jit(solution)/shard_map/expert_part/pallas_call | solution.py:518
  183.9 1.8 collective-permute-start.32
  186.1 2.6 %expert_part.3 = (bf16[24,7168]{1,0:T(8,128)(2,1)S(1)}, bf16[8,7168]{1,0:T(8,128)(2,1)S(1)}) custom-call(s32[5]{0:T(128)S(1)} %pad_add_fusion.where_ref, bf16[32,7296]{1,0:T(8,128)(2,1)S(1)} %collective-permute-done.30.refs_0_, bf16[7168,512]{1,0:T(8,128)(2,1)S(1)} %get-tuple-element.62.refs_3_.refs_1_, bf16[256,7168]{1,0:T(8,128)(2,1)S(1)} %get-tuple-element.63.refs_4_.refs_2_), custom_call_target="tpu_custom_call" | custom-call | flops 704643072 | bytes 458752 | tf_op jit(solution)/shard_map/expert_part/pallas_call | solution.py:518
  188.7 2.2 collective-permute-start.34
  190.9 0.9 plan.3.spread
  191.8 1.8 collective-permute-start.28
  193.9 3.7 %collective-permute-done.34.refs_3_ = bf16[24,7168]{1,0:T(8,128)(2,1)S(1)} collective-permute-done((bf16[24,7168]{1,0:T(8,128)(2,1)S(1)}, bf16[24,7168]{1,0:T(8,128)(2,1)S(1)}, u32[]{:S(2)}, u32[]{:S(2)}) %collective-permute-start.34) | collective-permute-done | bytes 344096 | tf_op jit(solution)/shard_map/ppermute | solution.py:39
  198.0 4.5 %collective-permute-start.35 = (bf16[32,3584]{1,0:T(8,128)(2,1)S(1)}, bf16[32,3584]{1,0:T(8,128)(2,1)S(1)}, u32[]{:S(2)}, u32[]{:S(2)}) collective-permute-start(bf16[32,3584]{1,0:T(8,128)(2,1)S(1)} %get-tuple-element.73), channel_id=1, source_target_pairs={{0,2},{2,4},{4,6},{6,8},{8,10},{10,12},{12,14},{14,16},{16,18},{18... | collective-permute-start | bytes 688136 | tf_op jit(solution)/shard_map/ppermute | solution.py:43
  202.5 3.0 %collective-permute-start.31 = (bf16[8,7168]{1,0:T(8,128)(2,1)S(1)}, bf16[8,7168]{1,0:T(8,128)(2,1)S(1)}, u32[]{:S(2)}, u32[]{:S(2)}) collective-permute-start(bf16[8,7168]{1,0:T(8,128)(2,1)S(1)} %get-tuple-element.68), channel_id=1, source_target_pairs={{0,64},{32,96},{64,0},{96,32},{1,65},{33,97},{65,1},{97,33},{2,66}... | collective-permute-start | bytes 344072 | tf_op jit(solution)/shard_map/ppermute | solution.py:39
  205.5 2.7 %collective-permute-start.37 = (bf16[32,1792]{1,0:T(8,128)(2,1)S(1)}, bf16[32,1792]{1,0:T(8,128)(2,1)S(1)}, u32[]{:S(2)}, u32[]{:S(2)}) collective-permute-start(bf16[32,1792]{1,0:T(8,128)(2,1)S(1)} %get-tuple-element.75), channel_id=1, source_target_pairs={{0,4},{2,6},{4,8},{6,10},{8,12},{10,14},{12,16},{14,18},{16,20},{1... | collective-permute-start | bytes 344072 | tf_op jit(solution)/shard_map/ppermute | solution.py:43
  208.2 1.5 collective-permute-start.38
  209.6 0.8 plan.2.refs_0_
  210.4 2.2 collective-permute-done.37.refs_7_
  212.6 3.0 %collective-permute-done.38.refs_8_ = bf16[32,1792]{1,0:T(8,128)(2,1)S(1)} collective-permute-done((bf16[32,1792]{1,0:T(8,128)(2,1)S(1)}, bf16[32,1792]{1,0:T(8,128)(2,1)S(1)}, u32[]{:S(2)}, u32[]{:S(2)}) %collective-permute-start.38) | collective-permute-done | bytes 114720 | tf_op jit(solution)/shard_map/ppermute | solution.py:43
  215.8 7.3 %collective-permute-start.39 = (bf16[8,3584]{1,0:T(8,128)(2,1)S(1)}, bf16[8,3584]{1,0:T(8,128)(2,1)S(1)}, u32[]{:S(2)}, u32[]{:S(2)}) collective-permute-start(bf16[8,3584]{1,0:T(8,128)(2,1)S(1)} %get-tuple-element.78), channel_id=1, source_target_pairs={{0,8},{8,0},{16,24},{24,16},{1,9},{9,1},{17,25},{25,17},{2,10},{10... | collective-permute-start | bytes 172040 | tf_op jit(solution)/shard_map/ppermute | solution.py:47
  223.1 5.5 %collective-permute-start.41 = (bf16[8,3584]{1,0:T(8,128)(2,1)S(1)}, bf16[8,3584]{1,0:T(8,128)(2,1)S(1)}, u32[]{:S(2)}, u32[]{:S(2)}) collective-permute-start(bf16[8,3584]{1,0:T(8,128)(2,1)S(1)} %get-tuple-element.80), channel_id=1, source_target_pairs={{0,24},{8,16},{16,8},{24,0},{1,25},{9,17},{17,9},{25,1},{2,26},{10... | collective-permute-start | bytes 172040 | tf_op jit(solution)/shard_map/ppermute | solution.py:47
  228.6 8.2 %collective-permute-done.40.two = bf16[8,3584]{1,0:T(8,128)(2,1)S(1)} collective-permute-done((bf16[8,3584]{1,0:T(8,128)(2,1)S(1)}, bf16[8,3584]{1,0:T(8,128)(2,1)S(1)}, u32[]{:S(2)}, u32[]{:S(2)}) %collective-permute-start.40) | collective-permute-done | bytes 57376 | tf_op jit(solution)/shard_map/ppermute | solution.py:47
  236.9 0.7 finish.1
  (64 shorter events, 2.7 us)
Async XLA Ops:
  3.9 161.8 %collective-permute-start.26 = (bf16[14336,128]{1,0:T(8,128)(2,1)}, bf16[14336,128]{1,0:T(8,128)(2,1)}, u32[]{:S(2)}, u32[]{:S(2)}) collective-permute-start(bf16[14336,128]{1,0:T(8,128)(2,1)} %pair.1), channel_id=1, source_target_pairs={{0,1},{1,0},{2,3},{3,2},{4,5},{5,4},{6,7},{7,6},{8,9},{9,8},{10,11... | collective-permute-start | bytes 11010056 | tf_op jit(solution)/shard_map/ppermute | solution.py:51
  5.2 14.2 %collective-permute-start.8 = (bf16[32,7680]{1,0:T(8,128)(2,1)S(1)}, bf16[32,7680]{1,0:T(8,128)(2,1)S(1)}, u32[]{:S(2)}, u32[]{:S(2)}) collective-permute-start(bf16[32,7680]{1,0:T(8,128)(2,1)S(1)} %get-tuple-element.43.refs_0_), channel_id=1, source_target_pairs={{0,96},{32,64},{64,32},{96,0},{1,97},{33,65},{65,33},{97,1},{2,98}... | collective-permute-start | bytes 1474568 | tf_op jit(solution)/shard_map/ppermute | solution.py:39
  5.8 14.2 %collective-permute-start = (bf16[32,7680]{1,0:T(8,128)(2,1)S(1)}, bf16[32,7680]{1,0:T(8,128)(2,1)}, u32[]{:S(2)}, u32[]{:S(2)}) collective-permute-start(bf16[32,7680]{1,0:T(8,128)(2,1)S(1)} %get-tuple-element.43.refs_0_), channel_id=1, source_target_pairs={{0,32},{32,0},{64,96},{96,64},{1,33},{33,1},{65,97},{97,65},{2,34}... | collective-permute-start | bytes 1474568 | tf_op jit(solution)/shard_map/ppermute | solution.py:39
  6.8 22.8 %collective-permute-start.7 = (bf16[32,7680]{1,0:T(8,128)(2,1)S(1)}, bf16[32,7680]{1,0:T(8,128)(2,1)S(1)}, u32[]{:S(2)}, u32[]{:S(2)}) collective-permute-start(bf16[32,7680]{1,0:T(8,128)(2,1)S(1)} %get-tuple-element.44.refs_1_), channel_id=1, source_target_pairs={{0,32},{32,0},{64,96},{96,64},{1,33},{33,1},{65,97},{97,65},{2,34}... | collective-permute-start | bytes 1474568 | tf_op jit(solution)/shard_map/ppermute | solution.py:39
  7.8 21.9 %collective-permute-start.2 = (bf16[32,7680]{1,0:T(8,128)(2,1)S(1)}, bf16[32,7680]{1,0:T(8,128)(2,1)S(1)}, u32[]{:S(2)}, u32[]{:S(2)}) collective-permute-start(bf16[32,7680]{1,0:T(8,128)(2,1)S(1)} %get-tuple-element.44.refs_1_), channel_id=1, source_target_pairs={{0,96},{32,64},{64,32},{96,0},{1,97},{33,65},{65,33},{97,1},{2,98}... | collective-permute-start | bytes 1474568 | tf_op jit(solution)/shard_map/ppermute | solution.py:39
  29.6 1.3 copy-start
  31.0 2.4 copy-start.6
  31.0 49.9 %collective-permute-start.9 = (bf16[128,7680]{1,0:T(8,128)(2,1)S(1)}, bf16[128,7680]{1,0:T(8,128)(2,1)}, u32[]{:S(2)}, u32[]{:S(2)}) collective-permute-start(bf16[128,7680]{1,0:T(8,128)(2,1)S(1)} %join.3.refs_2_), channel_id=1, source_target_pairs={{0,1},{1,0},{2,3},{3,2},{4,5},{5,4},{6,7},{7,6},{8,9},{9,8},{10,11... | collective-permute-start | bytes 5898248 | tf_op jit(solution)/shard_map/ppermute | solution.py:51
  31.2 31.1 %collective-permute-start.1 = (bf16[32,7680]{1,0:T(8,128)(2,1)}, bf16[32,7680]{1,0:T(8,128)(2,1)}, u32[]{:S(2)}, u32[]{:S(2)}) collective-permute-start(bf16[32,7680]{1,0:T(8,128)(2,1)} %collective-permute-done.refs_0_), channel_id=1, source_target_pairs={{0,96},{32,64},{64,32},{96,0},{1,97},{33,65},{65,33},{97,1},{2,98}... | collective-permute-start | bytes 1474568 | tf_op jit(solution)/shard_map/ppermute | solution.py:39
  33.1 43.7 %collective-permute-start.6 = (bf16[64,7680]{1,0:T(8,128)(2,1)S(1)}, bf16[64,7680]{1,0:T(8,128)(2,1)}, u32[]{:S(2)}, u32[]{:S(2)}) collective-permute-start(bf16[64,7680]{1,0:T(8,128)(2,1)S(1)} %join.2.refs_0_), channel_id=1, source_target_pairs={{0,1},{1,0},{2,3},{3,2},{4,5},{5,4},{6,7},{7,6},{8,9},{9,8},{10,11... | collective-permute-start | bytes 2949128 | tf_op jit(solution)/shard_map/ppermute | solution.py:51
  39.3 41.6 %all-to-all-start = ((bf16[16,16,512]{2,1,0:T(8,128)(2,1)}), bf16[16,16,512]{2,1,0:T(8,128)(2,1)S(1)}, u32[]{:S(2)}, u32[]{:S(2)}) async-start(bf16[16,16,512]{2,1,0:T(8,128)(2,1)} %bitcast.4), calls=%async_computation | async-start | bytes 524288 | tf_op jit(solution)/shard_map/all_to_all | solution.py:707
  62.2 103.4 %collective-permute-start.27 = (bf16[128,7168]{1,0:T(8,128)(2,1)}, bf16[128,7168]{1,0:T(8,128)(2,1)}, u32[]{:S(2)}, u32[]{:S(2)}) collective-permute-start(bf16[128,7168]{1,0:T(8,128)(2,1)} %down_a.1), channel_id=1, source_target_pairs={{0,1},{1,0},{2,3},{3,2},{4,5},{5,4},{6,7},{7,6},{8,9},{9,8},{10,11... | collective-permute-start | bytes 5505032 | tf_op jit(solution)/shard_map/ppermute | solution.py:51
  62.3 14.5 %collective-permute-start.3 = (bf16[32,7680]{1,0:T(8,128)(2,1)}, bf16[32,7680]{1,0:T(8,128)(2,1)}, u32[]{:S(2)}, u32[]{:S(2)}) collective-permute-start(bf16[32,7680]{1,0:T(8,128)(2,1)} %copy-done), channel_id=1, source_target_pairs={{0,32},{32,0},{64,96},{96,64},{1,33},{33,1},{65,97},{97,65},{2,34}... | collective-permute-start | bytes 1474568 | tf_op jit(solution)/shard_map/ppermute | solution.py:39
  76.8 7.4 %collective-permute-start.4 = (bf16[32,7680]{1,0:T(8,128)(2,1)}, bf16[32,7680]{1,0:T(8,128)(2,1)}, u32[]{:S(2)}, u32[]{:S(2)}) collective-permute-start(bf16[32,7680]{1,0:T(8,128)(2,1)} %collective-permute-done.1.refs_0_), channel_id=1, source_target_pairs={{0,1},{1,0},{2,3},{3,2},{4,5},{5,4},{6,7},{7,6},{8,9},{9,8},{10,11... | collective-permute-start | bytes 1474568 | tf_op jit(solution)/shard_map/ppermute | solution.py:51
  76.8 7.4 %collective-permute-start.5 = (bf16[32,7680]{1,0:T(8,128)(2,1)}, bf16[32,7680]{1,0:T(8,128)(2,1)}, u32[]{:S(2)}, u32[]{:S(2)}) collective-permute-start(bf16[32,7680]{1,0:T(8,128)(2,1)} %collective-permute-done.3.refs_1_), channel_id=1, source_target_pairs={{0,1},{1,0},{2,3},{3,2},{4,5},{5,4},{6,7},{7,6},{8,9},{9,8},{10,11... | collective-permute-start | bytes 1474568 | tf_op jit(solution)/shard_map/ppermute | solution.py:51
  84.1 29.7 %copy-start.3 = (bf16[7168]{0:T(1024)(128)(2,1)S(1)}, bf16[7168]{0:T(1024)(128)(2,1)}, u32[]{:S(2)}) copy-start(bf16[7168]{0:T(1024)(128)(2,1)} %param.21) | copy-start | bytes 43012
  84.2 29.7 %copy-start.2 = (bf16[2,2,7168]{2,1,0:T(2,128)(2,1)S(1)}, bf16[2,2,7168]{2,1,0:T(2,128)(2,1)}, u32[]{:S(2)}) copy-start(bf16[2,2,7168]{2,1,0:T(2,128)(2,1)} %param.18) | copy-start | bytes 172036
  84.2 35.6 %copy-start.4 = (s32[2,2,8]{2,1,0:T(2,128)S(1)}, s32[2,2,8]{2,1,0:T(2,128)}, u32[]{:S(2)}) copy-start(s32[2,2,8]{2,1,0:T(2,128)} %param.23) | copy-start | bytes 388
  84.2 35.6 %copy-start.5 = (s32[2,2,8]{2,1,0:T(2,128)S(1)}, s32[2,2,8]{2,1,0:T(2,128)}, u32[]{:S(2)}) copy-start(s32[2,2,8]{2,1,0:T(2,128)} %param.24) | copy-start | bytes 388
  86.6 33.2 %copy-start.1 = (bf16[7168,16]{0,1:T(8,128)(2,1)S(1)}, bf16[7168,16]{0,1:T(8,128)(2,1)}, u32[]{:S(2)}) copy-start(bf16[7168,16]{0,1:T(8,128)(2,1)} %param.22) | copy-start | bytes 688132
  86.6 9.3 %collective-permute-start.12 = (bf16[32,1792]{1,0:T(8,128)(2,1)S(1)}, bf16[32,1792]{1,0:T(8,128)(2,1)S(1)}, u32[]{:S(2)}, u32[]{:S(2)}) collective-permute-start(bf16[32,1792]{1,0:T(8,128)(2,1)S(1)} %get-tuple-element.48), channel_id=1, source_target_pairs={{0,4},{2,6},{4,8},{6,10},{8,12},{10,14},{12,16},{14,18},{16,20},{1... | collective-permute-start | bytes 344072 | tf_op jit(solution)/shard_map/ppermute | solution.py:43
  89.0 13.3 %collective-permute-start.10 = (bf16[32,3584]{1,0:T(8,128)(2,1)S(1)}, bf16[32,3584]{1,0:T(8,128)(2,1)S(1)}, u32[]{:S(2)}, u32[]{:S(2)}) collective-permute-start(bf16[32,3584]{1,0:T(8,128)(2,1)S(1)} %get-tuple-element.46), channel_id=1, source_target_pairs={{0,2},{2,4},{4,6},{6,8},{8,10},{10,12},{12,14},{14,16},{16,18},{18... | collective-permute-start | bytes 688136 | tf_op jit(solution)/shard_map/ppermute | solution.py:43
  89.2 13.1 %collective-permute-start.11 = (bf16[32,3584]{1,0:T(8,128)(2,1)S(1)}, bf16[32,3584]{1,0:T(8,128)(2,1)S(1)}, u32[]{:S(2)}, u32[]{:S(2)}) collective-permute-start(bf16[32,3584]{1,0:T(8,128)(2,1)S(1)} %get-tuple-element.47), channel_id=1, source_target_pairs={{0,30},{2,0},{4,2},{6,4},{8,6},{10,8},{12,10},{14,12},{16,14},{18,... | collective-permute-start | bytes 688136 | tf_op jit(solution)/shard_map/ppermute | solution.py:43
  96.0 6.3 %collective-permute-start.13 = (bf16[32,1792]{1,0:T(8,128)(2,1)S(1)}, bf16[32,1792]{1,0:T(8,128)(2,1)S(1)}, u32[]{:S(2)}, u32[]{:S(2)}) collective-permute-start(bf16[32,1792]{1,0:T(8,128)(2,1)S(1)} %get-tuple-element.49), channel_id=1, source_target_pairs={{0,28},{2,30},{4,0},{6,2},{8,4},{10,6},{12,8},{14,10},{16,12},{18,... | collective-permute-start | bytes 344072 | tf_op jit(solution)/shard_map/ppermute | solution.py:43
  102.4 11.6 %collective-permute-start.14 = (bf16[8,3584]{1,0:T(8,128)(2,1)S(1)}, bf16[8,3584]{1,0:T(8,128)(2,1)S(1)}, u32[]{:S(2)}, u32[]{:S(2)}) collective-permute-start(bf16[8,3584]{1,0:T(8,128)(2,1)S(1)} %get-tuple-element.51), channel_id=1, source_target_pairs={{0,8},{8,0},{16,24},{24,16},{1,9},{9,1},{17,25},{25,17},{2,10},{10... | collective-permute-start | bytes 172040 | tf_op jit(solution)/shard_map/ppermute | solution.py:47
  104.6 14.3 %collective-permute-start.15 = (bf16[8,3584]{1,0:T(8,128)(2,1)S(1)}, bf16[8,3584]{1,0:T(8,128)(2,1)S(1)}, u32[]{:S(2)}, u32[]{:S(2)}) collective-permute-start(bf16[8,3584]{1,0:T(8,128)(2,1)S(1)} %get-tuple-element.52), channel_id=1, source_target_pairs={{0,16},{8,24},{16,0},{24,8},{1,17},{9,25},{17,1},{25,9},{2,18},{10... | collective-permute-start | bytes 172040 | tf_op jit(solution)/shard_map/ppermute | solution.py:47
  111.4 8.5 %collective-permute-start.16 = (bf16[8,3584]{1,0:T(8,128)(2,1)S(1)}, bf16[8,3584]{1,0:T(8,128)(2,1)S(1)}, u32[]{:S(2)}, u32[]{:S(2)}) collective-permute-start(bf16[8,3584]{1,0:T(8,128)(2,1)S(1)} %get-tuple-element.53), channel_id=1, source_target_pairs={{0,24},{8,16},{16,8},{24,0},{1,25},{9,17},{17,9},{25,1},{2,26},{10... | collective-permute-start | bytes 172040 | tf_op jit(solution)/shard_map/ppermute | solution.py:47
  120.5 11.4 %collective-permute-start.19 = (bf16[8,3712]{1,0:T(8,128)(2,1)S(1)}, bf16[8,3712]{1,0:T(8,128)(2,1)S(1)}, u32[]{:S(2)}, u32[]{:S(2)}) collective-permute-start(bf16[8,3712]{1,0:T(8,128)(2,1)S(1)} %get-tuple-element.55.refs_0_), channel_id=1, source_target_pairs={{0,24},{8,16},{16,8},{24,0},{1,25},{9,17},{17,9},{25,1},{2,26},{10... | collective-permute-start | bytes 178184 | tf_op jit(solution)/shard_map/ppermute | solution.py:47
  125.0 13.4 %collective-permute-start.18 = (bf16[8,3712]{1,0:T(8,128)(2,1)S(1)}, bf16[8,3712]{1,0:T(8,128)(2,1)S(1)}, u32[]{:S(2)}, u32[]{:S(2)}) collective-permute-start(bf16[8,3712]{1,0:T(8,128)(2,1)S(1)} %get-tuple-element.55.refs_0_), channel_id=1, source_target_pairs={{0,16},{8,24},{16,0},{24,8},{1,17},{9,25},{17,1},{25,9},{2,18},{10... | collective-permute-start | bytes 178184 | tf_op jit(solution)/shard_map/ppermute | solution.py:47
  131.4 10.3 %collective-permute-start.17 = (bf16[8,3712]{1,0:T(8,128)(2,1)S(1)}, bf16[8,3712]{1,0:T(8,128)(2,1)S(1)}, u32[]{:S(2)}, u32[]{:S(2)}) collective-permute-start(bf16[8,3712]{1,0:T(8,128)(2,1)S(1)} %get-tuple-element.55.refs_0_), channel_id=1, source_target_pairs={{0,8},{8,0},{16,24},{24,16},{1,9},{9,1},{17,25},{25,17},{2,10},{10... | collective-permute-start | bytes 178184 | tf_op jit(solution)/shard_map/ppermute | solution.py:47
  142.2 9.6 %collective-permute-start.21 = (bf16[16,3712]{1,0:T(8,128)(2,1)S(1)}, bf16[16,3712]{1,0:T(8,128)(2,1)S(1)}, u32[]{:S(2)}, u32[]{:S(2)}) collective-permute-start(bf16[16,3712]{1,0:T(8,128)(2,1)S(1)} %get-tuple-element.57), channel_id=1, source_target_pairs={{0,28},{2,30},{4,0},{6,2},{8,4},{10,6},{12,8},{14,10},{16,12},{18,... | collective-permute-start | bytes 356360 | tf_op jit(solution)/shard_map/ppermute | solution.py:43
  145.8 13.0 %collective-permute-start.23 = (bf16[32,3712]{1,0:T(8,128)(2,1)S(1)}, bf16[32,3712]{1,0:T(8,128)(2,1)S(1)}, u32[]{:S(2)}, u32[]{:S(2)}) collective-permute-start(bf16[32,3712]{1,0:T(8,128)(2,1)S(1)} %get-tuple-element.56.refs_0_.refs_4_), channel_id=1, source_target_pairs={{0,2},{2,4},{4,6},{6,8},{8,10},{10,12},{12,14},{14,16},{16,18},{18... | collective-permute-start | bytes 712712 | tf_op jit(solution)/shard_map/ppermute | solution.py:43
  145.9 12.9 %collective-permute-start.20 = (bf16[32,3712]{1,0:T(8,128)(2,1)S(1)}, bf16[32,3712]{1,0:T(8,128)(2,1)S(1)}, u32[]{:S(2)}, u32[]{:S(2)}) collective-permute-start(bf16[32,3712]{1,0:T(8,128)(2,1)S(1)} %get-tuple-element.56.refs_0_.refs_4_), channel_id=1, source_target_pairs={{0,30},{2,0},{4,2},{6,4},{8,6},{10,8},{12,10},{14,12},{16,14},{18,... | collective-permute-start | bytes 712712 | tf_op jit(solution)/shard_map/ppermute | solution.py:43
  151.8 6.9 %collective-permute-start.22 = (bf16[16,3712]{1,0:T(8,128)(2,1)S(1)}, bf16[16,3712]{1,0:T(8,128)(2,1)S(1)}, u32[]{:S(2)}, u32[]{:S(2)}) collective-permute-start(bf16[16,3712]{1,0:T(8,128)(2,1)S(1)} %get-tuple-element.58), channel_id=1, source_target_pairs={{0,4},{2,6},{4,8},{6,10},{8,12},{10,14},{12,16},{14,18},{16,20},{1... | collective-permute-start | bytes 356360 | tf_op jit(solution)/shard_map/ppermute | solution.py:43
  160.1 11.2 %collective-permute-start.24 = (bf16[32,7296]{1,0:T(8,128)(2,1)S(1)}, bf16[32,7296]{1,0:T(8,128)(2,1)S(1)}, u32[]{:S(2)}, u32[]{:S(2)}) collective-permute-start(bf16[32,7296]{1,0:T(8,128)(2,1)S(1)} %get-tuple-element.60), channel_id=1, source_target_pairs={{0,32},{32,0},{64,96},{96,64},{1,33},{33,1},{65,97},{97,65},{2,34}... | collective-permute-start | bytes 1400840 | tf_op jit(solution)/shard_map/ppermute | solution.py:39
  163.4 18.0 %collective-permute-start.25 = (bf16[32,7296]{1,0:T(8,128)(2,1)S(1)}, bf16[32,7296]{1,0:T(8,128)(2,1)S(1)}, u32[]{:S(2)}, u32[]{:S(2)}) collective-permute-start(bf16[32,7296]{1,0:T(8,128)(2,1)S(1)} %get-tuple-element.61), channel_id=1, source_target_pairs={{0,96},{32,64},{64,32},{96,0},{1,97},{33,65},{65,33},{97,1},{2,98}... | collective-permute-start | bytes 1400840 | tf_op jit(solution)/shard_map/ppermute | solution.py:39
  163.4 22.7 %collective-permute-start.30 = (bf16[32,7296]{1,0:T(8,128)(2,1)S(1)}, bf16[32,7296]{1,0:T(8,128)(2,1)S(1)}, u32[]{:S(2)}, u32[]{:S(2)}) collective-permute-start(bf16[32,7296]{1,0:T(8,128)(2,1)S(1)} %get-tuple-element.67), channel_id=1, source_target_pairs={{0,64},{32,96},{64,0},{96,32},{1,65},{33,97},{65,1},{97,33},{2,66}... | collective-permute-start | bytes 1400840 | tf_op jit(solution)/shard_map/ppermute | solution.py:39
  183.9 10.0 %collective-permute-start.32 = (bf16[24,7168]{1,0:T(8,128)(2,1)S(1)}, bf16[24,7168]{1,0:T(8,128)(2,1)S(1)}, u32[]{:S(2)}, u32[]{:S(2)}) collective-permute-start(bf16[24,7168]{1,0:T(8,128)(2,1)S(1)} %get-tuple-element.70), channel_id=1, source_target_pairs={{0,32},{32,0},{64,96},{96,64},{1,33},{33,1},{65,97},{97,65},{2,34}... | collective-permute-start | bytes 1032200 | tf_op jit(solution)/shard_map/ppermute | solution.py:39
  185.7 8.2 %collective-permute-start.33 = (bf16[24,7168]{1,0:T(8,128)(2,1)S(1)}, bf16[24,7168]{1,0:T(8,128)(2,1)S(1)}, u32[]{:S(2)}, u32[]{:S(2)}) collective-permute-start(bf16[24,7168]{1,0:T(8,128)(2,1)S(1)} %get-tuple-element.71), channel_id=1, source_target_pairs={{0,96},{32,64},{64,32},{96,0},{1,97},{33,65},{65,33},{97,1},{2,98}... | collective-permute-start | bytes 1032200 | tf_op jit(solution)/shard_map/ppermute | solution.py:39
  188.7 8.9 %collective-permute-start.34 = (bf16[24,7168]{1,0:T(8,128)(2,1)S(1)}, bf16[24,7168]{1,0:T(8,128)(2,1)S(1)}, u32[]{:S(2)}, u32[]{:S(2)}) collective-permute-start(bf16[24,7168]{1,0:T(8,128)(2,1)S(1)} %get-tuple-element.72), channel_id=1, source_target_pairs={{0,64},{32,96},{64,0},{96,32},{1,65},{33,97},{65,1},{97,33},{2,66}... | collective-permute-start | bytes 1032200 | tf_op jit(solution)/shard_map/ppermute | solution.py:39
  191.8 13.7 %collective-permute-start.28 = (bf16[8,7168]{1,0:T(8,128)(2,1)S(1)}, bf16[8,7168]{1,0:T(8,128)(2,1)S(1)}, u32[]{:S(2)}, u32[]{:S(2)}) collective-permute-start(bf16[8,7168]{1,0:T(8,128)(2,1)S(1)} %get-tuple-element.65), channel_id=1, source_target_pairs={{0,32},{32,0},{64,96},{96,64},{1,33},{33,1},{65,97},{97,65},{2,34}... | collective-permute-start | bytes 344072 | tf_op jit(solution)/shard_map/ppermute | solution.py:39
  193.5 14.6 %collective-permute-start.29 = (bf16[8,7168]{1,0:T(8,128)(2,1)S(1)}, bf16[8,7168]{1,0:T(8,128)(2,1)S(1)}, u32[]{:S(2)}, u32[]{:S(2)}) collective-permute-start(bf16[8,7168]{1,0:T(8,128)(2,1)S(1)} %get-tuple-element.66), channel_id=1, source_target_pairs={{0,96},{32,64},{64,32},{96,0},{1,97},{33,65},{65,33},{97,1},{2,98}... | collective-permute-start | bytes 344072 | tf_op jit(solution)/shard_map/ppermute | solution.py:39
  198.0 17.6 %collective-permute-start.35 = (bf16[32,3584]{1,0:T(8,128)(2,1)S(1)}, bf16[32,3584]{1,0:T(8,128)(2,1)S(1)}, u32[]{:S(2)}, u32[]{:S(2)}) collective-permute-start(bf16[32,3584]{1,0:T(8,128)(2,1)S(1)} %get-tuple-element.73), channel_id=1, source_target_pairs={{0,2},{2,4},{4,6},{6,8},{8,10},{10,12},{12,14},{14,16},{16,18},{18... | collective-permute-start | bytes 688136 | tf_op jit(solution)/shard_map/ppermute | solution.py:43
  202.5 13.1 %collective-permute-start.36 = (bf16[32,3584]{1,0:T(8,128)(2,1)S(1)}, bf16[32,3584]{1,0:T(8,128)(2,1)S(1)}, u32[]{:S(2)}, u32[]{:S(2)}) collective-permute-start(bf16[32,3584]{1,0:T(8,128)(2,1)S(1)} %get-tuple-element.74), channel_id=1, source_target_pairs={{0,30},{2,0},{4,2},{6,4},{8,6},{10,8},{12,10},{14,12},{16,14},{18,... | collective-permute-start | bytes 688136 | tf_op jit(solution)/shard_map/ppermute | solution.py:43
  202.5 7.9 %collective-permute-start.31 = (bf16[8,7168]{1,0:T(8,128)(2,1)S(1)}, bf16[8,7168]{1,0:T(8,128)(2,1)S(1)}, u32[]{:S(2)}, u32[]{:S(2)}) collective-permute-start(bf16[8,7168]{1,0:T(8,128)(2,1)S(1)} %get-tuple-element.68), channel_id=1, source_target_pairs={{0,64},{32,96},{64,0},{96,32},{1,65},{33,97},{65,1},{97,33},{2,66}... | collective-permute-start | bytes 344072 | tf_op jit(solution)/shard_map/ppermute | solution.py:39
  205.5 7.1 %collective-permute-start.37 = (bf16[32,1792]{1,0:T(8,128)(2,1)S(1)}, bf16[32,1792]{1,0:T(8,128)(2,1)S(1)}, u32[]{:S(2)}, u32[]{:S(2)}) collective-permute-start(bf16[32,1792]{1,0:T(8,128)(2,1)S(1)} %get-tuple-element.75), channel_id=1, source_target_pairs={{0,4},{2,6},{4,8},{6,10},{8,12},{10,14},{12,16},{14,18},{16,20},{1... | collective-permute-start | bytes 344072 | tf_op jit(solution)/shard_map/ppermute | solution.py:43
  208.2 7.4 %collective-permute-start.38 = (bf16[32,1792]{1,0:T(8,128)(2,1)S(1)}, bf16[32,1792]{1,0:T(8,128)(2,1)S(1)}, u32[]{:S(2)}, u32[]{:S(2)}) collective-permute-start(bf16[32,1792]{1,0:T(8,128)(2,1)S(1)} %get-tuple-element.76), channel_id=1, source_target_pairs={{0,28},{2,30},{4,0},{6,2},{8,4},{10,6},{12,8},{14,10},{16,12},{18,... | collective-permute-start | bytes 344072 | tf_op jit(solution)/shard_map/ppermute | solution.py:43
  215.8 12.8 %collective-permute-start.39 = (bf16[8,3584]{1,0:T(8,128)(2,1)S(1)}, bf16[8,3584]{1,0:T(8,128)(2,1)S(1)}, u32[]{:S(2)}, u32[]{:S(2)}) collective-permute-start(bf16[8,3584]{1,0:T(8,128)(2,1)S(1)} %get-tuple-element.78), channel_id=1, source_target_pairs={{0,8},{8,0},{16,24},{24,16},{1,9},{9,1},{17,25},{25,17},{2,10},{10... | collective-permute-start | bytes 172040 | tf_op jit(solution)/shard_map/ppermute | solution.py:47
  223.1 13.7 %collective-permute-start.40 = (bf16[8,3584]{1,0:T(8,128)(2,1)S(1)}, bf16[8,3584]{1,0:T(8,128)(2,1)S(1)}, u32[]{:S(2)}, u32[]{:S(2)}) collective-permute-start(bf16[8,3584]{1,0:T(8,128)(2,1)S(1)} %get-tuple-element.79), channel_id=1, source_target_pairs={{0,16},{8,24},{16,0},{24,8},{1,17},{9,25},{17,1},{25,9},{2,18},{10... | collective-permute-start | bytes 172040 | tf_op jit(solution)/shard_map/ppermute | solution.py:47
  223.1 13.7 %collective-permute-start.41 = (bf16[8,3584]{1,0:T(8,128)(2,1)S(1)}, bf16[8,3584]{1,0:T(8,128)(2,1)S(1)}, u32[]{:S(2)}, u32[]{:S(2)}) collective-permute-start(bf16[8,3584]{1,0:T(8,128)(2,1)S(1)} %get-tuple-element.80), channel_id=1, source_target_pairs={{0,24},{8,16},{16,8},{24,0},{1,25},{9,17},{17,9},{25,1},{2,26},{10... | collective-permute-start | bytes 172040 | tf_op jit(solution)/shard_map/ppermute | solution.py:47
